TPU v7x, 16 devices: a 4x2x1 block of a 4x4x8 slice. The times are simulated.
16 devices in a mesh: rep: 2 (over y, z), dp: 8 (over x, core).
Axes of the slice: x: 4, y: 2, z: 1, core: 2. Of those that a mesh axis runs over, the one named last changes fastest.
The devices are a block of a 4x4x8 slice.
Arguments:
- x: bfloat16 [16, 1024, 1024], P(('rep', 'dp')), parts along dimension 0
- dy: bfloat16 [16, 1024, 1024], P(('rep', 'dp')), parts along dimension 0
- w_gate: bfloat16 [2, 1024, 3200], replicated
- w_up: bfloat16 [2, 1024, 3200], replicated
- w_down: bfloat16 [2, 3200, 1024], replicated
- m_w_gate: float32 [2, 1024, 3200], replicated
- m_w_up: float32 [2, 1024, 3200], replicated
- m_w_down: float32 [2, 3200, 1024], replicated
- v_w_gate: float32 [2, 1024, 3200], replicated
- v_w_up: float32 [2, 1024, 3200], replicated
- v_w_down: float32 [2, 3200, 1024], replicated
Outputs:
- output 1: bfloat16 [4, 1024, 3200], P('rep'), parts along dimension 0
- output 2: bfloat16 [4, 1024, 3200], P('rep'), parts along dimension 0
- output 3: bfloat16 [4, 3200, 1024], P('rep'), parts along dimension 0
- output 4: float32 [4, 1024, 3200], P('rep'), parts along dimension 0
- output 5: float32 [4, 1024, 3200], P('rep'), parts along dimension 0
- output 6: float32 [4, 3200, 1024], P('rep'), parts along dimension 0
- output 7: float32 [4, 1024, 3200], P('rep'), parts along dimension 0
- output 8: float32 [4, 1024, 3200], P('rep'), parts along dimension 0
- output 9: float32 [4, 3200, 1024], P('rep'), parts along dimension 0
There are 2 independent parts. A program takes and returns all parts, laid end to end along the dimension named above; an argument that names none is the same for every part.
All inputs are finite; a program needn't handle non-finite values.
Results may differ from a plain program's by a relative error of at most 0.022.
Values are sent between devices in bfloat16 or wider.
A program may use at most 768 MiB of HBM per device.

v0:
```python
import jax
import jax.numpy as jnp
from jax import lax
from jax.sharding import PartitionSpec as P

NAMES = ("w_gate", "w_up", "w_down")


def matmul(a, w):
    return jnp.dot(a, w, preferred_element_type=jnp.float32).astype(jnp.bfloat16)


def normed(h):
    wide = h.astype(jnp.float32)
    scale = lax.rsqrt(jnp.mean(wide**2, -1, keepdims=True) + 1e-6)
    return (wide * scale).astype(jnp.bfloat16)


def layer(h, w):
    a = normed(h)
    gate = jnp.dot(a, w["w_gate"], preferred_element_type=jnp.float32)
    up = jnp.dot(a, w["w_up"], preferred_element_type=jnp.float32)
    return h + matmul((jax.nn.silu(gate) * up).astype(jnp.bfloat16), w["w_down"])


def adamw(w, m, v, g):
    m = 0.9 * m + 0.1 * g
    v = 0.95 * v + 0.05 * g * g
    step = m * lax.rsqrt(v + 1e-8) + 0.1 * w
    return (w - 0.02 * step).astype(jnp.bfloat16), m, v


def clipped(gradients, sum_of_squares, count):
    factor = jnp.minimum(1.0, 0.5 * lax.rsqrt(sum_of_squares / count + 1e-30))
    return [g * factor for g in gradients]


def solution(mesh):
    def step(x, dy, *arrays):
        weights, m, v = (arrays[i : i + 3] for i in (0, 3, 6))
        layers = weights[0].shape[0]
        h, kept = x[0], []
        for number in range(layers):
            kept.append(h)
            h = layer(h, {name: w[number] for name, w in zip(NAMES, weights, strict=True)})
        by_h, summed = dy[0], [None] * layers
        for number in reversed(range(layers)):
            _, back = jax.vjp(lambda w, h: layer(h, w), {name: w[number] for name, w in zip(NAMES, weights, strict=True)}, kept[number])
            by_w, by_h = back(by_h)
            summed[number] = [lax.psum(by_w[name], "dp") for name in NAMES]
        gradients = [jnp.stack([summed[number][i] for number in range(layers)]).astype(jnp.float32) for i in range(3)]
        gradients = clipped(gradients, sum(jnp.sum(g * g) for g in gradients), sum(g.size for g in gradients))
        new = [adamw(w.astype(jnp.float32), m, v, g) for w, m, v, g in zip(weights, m, v, gradients, strict=True)]
        return tuple(one[which] for which in range(3) for one in new)

    return jax.shard_map(
        step,
        mesh=mesh,
        in_specs=(P(("rep", "dp"), None, None),) * 2 + (P(None, None, None),) * 9,
        out_specs=(P("rep", None, None),) * 9,
        check_vma=False,
    )
```

profile of v0, /device:TPU:112, one launch (start us, length us, event | category | flops | bytes accessed | tf_op | source)
XLA Modules:
  0.0 800.1 jit_solution(4004454127102224473)
XLA Ops:
  7.3 2.9 copy.20
  10.6 4.2 copy.21
  14.8 12.5 %convolution_convert_fusion.4 = bf16[1024,3200]{1,0:T(8,128)(2,1)} fusion(bf16[2,3200,1024]{2,1,0:T(8,128)(2,1)} %param.15, bf16[1,1024,1024]{2,1,0:T(8,128)(2,1)} %param.12), kind=kOutput, calls=%fused_computation.68 | convolution fusion | flops 6714163200 | bytes 15204352 | tf_op jit(solution)/shard_map/transpose(jvp())/dot_general | solution.py:10
  27.4 10.5 %fusion.52 = f32[1024,3200]{1,0:T(8,128)} fusion(bf16[2,1024,3200]{2,1,0:T(8,128)(2,1)S(1)} %bitcast.77, bf16[1,1024,1024]{2,1,0:T(8,128)(2,1)S(1)} %copy-done.5, f32[1024]{0:T(1024)S(1)} %add_rsqrt_fusion), kind=kOutput, calls=%fused_computation.86 | convolution fusion | flops 6714032128 | bytes 21762048 | tf_op jit(solution)/shard_map/dot_general | solution.py:21
  37.9 16.7 %multiply_convert_fusion.1 = (bf16[1024,3200]{1,0:T(8,128)(2,1)}, f32[1024,3200]{1,0:T(8,128)}) fusion(f32[1024,3200]{1,0:T(8,128)} %fusion.52, bf16[2,1024,3200]{2,1,0:T(8,128)(2,1)} %param.14, bf16[1,1024,1024]{2,1,0:T(8,128)(2,1)} %param.11, f32[1024]{0:T(1024)S(1)} %add_rsqrt_fusion), kind=kOutput, calls=%fused_computation.56 | convolution fusion | flops 6733692928 | bytes 41422848 | tf_op jit(solution)/shard_map/dot_general | solution.py:22
  54.6 11.6 %fusion.76 = (f32[1024]{0:T(1024)S(1)}, bf16[1024,1024]{0,1:T(8,128)(2,1)S(1)}) fusion(bf16[1024,3200]{1,0:T(8,128)(2,1)} %get-tuple-element.24, bf16[2,3200,1024]{2,1,0:T(8,128)(2,1)} %param.15, bf16[1,1024,1024]{1,2,0:T(8,128)(2,1)S(1)} %copy.20), kind=kOutput, calls=%fused_computation.111 | convolution fusion | flops 6716128256 | bytes 17305600 | tf_op jit(solution)/shard_map/dot_general | solution.py:10
  67.5 13.2 %fusion.39 = f32[1024,3200]{1,0:T(8,128)} fusion(bf16[2,1024,3200]{2,1,0:T(8,128)(2,1)} %param.14, bf16[1024,1024]{0,1:T(8,128)(2,1)S(1)} %get-tuple-element.27, f32[1024]{0:T(1024)S(1)} %fusion.96), kind=kOutput, calls=%fused_computation.73 | convolution fusion | flops 6714032128 | bytes 21762048 | tf_op jit(solution)/shard_map/jvp()/dot_general | solution.py:22
  80.8 23.4 %fusion.23 = (bf16[1024,3200]{1,0:T(8,128)(2,1)}, f32[1024,3200]{1,0:T(8,128)}) fusion(f32[1024,3200]{1,0:T(8,128)} %fusion.39, bf16[1024,3200]{1,0:T(8,128)(2,1)} %convolution_convert_fusion.4, bf16[2,1024,3200]{2,1,0:T(8,128)(2,1)} %param.13, bf16[1024,1024]{0,1:T(8,128)(2,1)} %copy-done.3, f32[1024]{0:T(1024)S(1)} %fusion.96), kind=kOutput, calls=%fused_computation.44 | convolution fusion | flops 6753353728 | bytes 47976448 | tf_op jit(solution)/shard_map/jvp()/dot_general | solution.py:21
  104.2 13.5 %fusion.33 = bf16[1024,1024]{0,1:T(8,128)(2,1)S(1)} fusion(bf16[1024,3200]{1,0:T(8,128)(2,1)} %convolution_convert_fusion.4, bf16[2,1024,3200]{2,1,0:T(8,128)(2,1)} %param.14, f32[1024,3200]{1,0:T(8,128)} %get-tuple-element.29), kind=kOutput, calls=%fused_computation.60 | convolution fusion | flops 6730547200 | bytes 28311552 | tf_op jit(solution)/shard_map/transpose(jvp())/dot_general | solution.py:22
  117.7 14.6 %fusion.65 = bf16[1,1024,3200]{2,1,0:T(8,128)(2,1)} fusion(bf16[1024,3200]{1,0:T(8,128)(2,1)} %convolution_convert_fusion.4, bf16[1024,1024]{0,1:T(8,128)(2,1)S(1)} %copy-done.4, f32[1024]{0:T(1024)S(1)} %fusion.96, f32[1024,3200]{1,0:T(8,128)} %get-tuple-element.29), kind=kOutput, calls=%fused_computation.97 | convolution fusion | flops 6736969728 | bytes 28315648 | tf_op jit(solution)/shard_map/transpose(jvp())/dot_general | solution.py:22
  132.4 14.7 %fusion.60 = bf16[1,3200,1024]{2,1,0:T(8,128)(2,1)} fusion(f32[1024,3200]{1,0:T(8,128)} %fusion.39, bf16[1,1024,1024]{2,1,0:T(8,128)(2,1)S(1)} %copy-done.6, f32[1024,3200]{1,0:T(8,128)} %get-tuple-element.29), kind=kOutput, calls=%fused_computation.94 | convolution fusion | flops 6733824000 | bytes 34865152 | tf_op jit(solution)/shard_map/transpose(jvp())/dot_general | solution.py:10
  147.1 12.1 %fusion.58 = bf16[1,1024,3200]{2,1,0:T(8,128)(2,1)} fusion(bf16[1024,3200]{1,0:T(8,128)(2,1)} %get-tuple-element.28, bf16[1024,1024]{0,1:T(8,128)(2,1)S(1)} %copy-done.4, f32[1024]{0:T(1024)S(1)} %fusion.96), kind=kOutput, calls=%fused_computation.92 | convolution fusion | flops 6714032128 | bytes 15208448 | tf_op jit(solution)/shard_map/transpose(jvp())/dot_general | solution.py:21
  159.1 11.8 %fusion.78 = (f32[1024]{0:T(1024)S(1)}, bf16[1024,1024]{0,1:T(8,128)(2,1)S(1)}) fusion(bf16[1024,1024]{0,1:T(8,128)(2,1)S(1)} %copy-done.4, bf16[1024,1024]{0,1:T(8,128)(2,1)S(1)} %fusion.33, bf16[1024,3200]{1,0:T(8,128)(2,1)} %get-tuple-element.28, bf16[2,1024,3200]{2,1,0:T(8,128)(2,1)} %param.13), kind=kOutput, calls=%fused_computation.113 | convolution fusion | flops 6716128256 | bytes 19402752 | tf_op jit(solution)/shard_map/transpose(jvp())/dot_general | solution.py:21
  171.0 1.6 fusion.81
  172.6 9.3 %convolution_convert_fusion.3 = bf16[1024,3200]{1,0:T(8,128)(2,1)} fusion(bf16[1024,1024]{0,1:T(8,128)(2,1)S(1)} %fusion.81, bf16[2,3200,1024]{2,1,0:T(8,128)(2,1)S(1)} %bitcast.75), kind=kOutput, calls=%fused_computation.67 | convolution fusion | flops 6714163200 | bytes 15204352 | tf_op jit(solution)/shard_map/transpose(jvp())/dot_general | solution.py:10
  182.0 12.0 %fusion.59 = bf16[1,3200,1024]{2,1,0:T(8,128)(2,1)} fusion(bf16[1024,3200]{1,0:T(8,128)(2,1)} %get-tuple-element.24, bf16[1024,1024]{0,1:T(8,128)(2,1)S(1)} %fusion.81), kind=kOutput, calls=%fused_computation.93 | convolution fusion | flops 6714163200 | bytes 15204352 | tf_op jit(solution)/shard_map/transpose(jvp())/dot_general | solution.py:10
  194.0 13.3 %fusion.61 = bf16[1,1024,3200]{2,1,0:T(8,128)(2,1)} fusion(bf16[1024,3200]{1,0:T(8,128)(2,1)S(1)} %copy-done.11, f32[1024,3200]{1,0:T(8,128)} %fusion.52, bf16[1,1024,1024]{1,2,0:T(8,128)(2,1)S(1)} %copy-done.2, f32[1024]{0:T(1024)S(1)} %copy-done.10), kind=kOutput, calls=%fused_computation.95 | convolution fusion | flops 6736969728 | bytes 28315648 | tf_op jit(solution)/shard_map/transpose(jvp())/dot_general | solution.py:22
  207.3 16.9 %fusion.62 = bf16[1,1024,3200]{2,1,0:T(8,128)(2,1)} fusion(f32[1024,3200]{1,0:T(8,128)} %fusion.52, f32[1024,3200]{1,0:T(8,128)} %get-tuple-element.25, bf16[1024,3200]{1,0:T(8,128)(2,1)} %convolution_convert_fusion.3, bf16[1,1024,1024]{1,2,0:T(8,128)(2,1)S(1)} %copy-done.2, f32[1024]{0:T(1024)S(1)} %copy-done.10), kind=kOutput, calls=%fused_computation.96 | convolution fusion | flops 6753353728 | bytes 41422848 | tf_op jit(solution)/shard_map/transpose(jvp())/dot_general | solution.py:21
  224.3 389.3 %all-reduce.3.cloned.1.call-done = (bf16[1,1024,3200]{2,1,0:T(8,128)(2,1)}, bf16[1,1024,3200]{2,1,0:T(8,128)(2,1)}, bf16[1,1024,3200]{2,1,0:T(8,128)(2,1)}, bf16...) async-done(((bf16[1,1024,3200]{2,1,0:T(8,128)(2,1)}, bf16[1,1024,3200]{2,1,0:T(8,128)(2,1)}, ...) | async-done | bytes 39321616 | tf_op jit(solution)/shard_map/psum | solution.py:50
  613.5 12.1 %fusion.9 = f32[]{:T(128)} fusion(bf16[1,1024,3200]{2,1,0:T(8,128)(2,1)} %get-tuple-element.9, bf16[1,1024,3200]{2,1,0:T(8,128)(2,1)} %get-tuple-element.10), kind=kLoop, calls=%fused_computation.24 | loop fusion | flops 26214400 | bytes 13107204 | tf_op jit(solution)/shard_map/reduce_sum | solution.py:52
  625.6 12.1 %fusion.10 = f32[]{:T(128)} fusion(bf16[1,1024,3200]{2,1,0:T(8,128)(2,1)} %get-tuple-element.11, bf16[1,1024,3200]{2,1,0:T(8,128)(2,1)} %get-tuple-element.12), kind=kLoop, calls=%fused_computation.25 | loop fusion | flops 26214400 | bytes 13107204 | tf_op jit(solution)/shard_map/reduce_sum | solution.py:52
  639.0 12.2 %fusion.11 = f32[]{:T(128)} fusion(bf16[1,3200,1024]{2,1,0:T(8,128)(2,1)} %get-tuple-element.13, bf16[1,3200,1024]{2,1,0:T(8,128)(2,1)} %get-tuple-element.14), kind=kLoop, calls=%fused_computation.26 | loop fusion | flops 26214400 | bytes 13107204 | tf_op jit(solution)/shard_map/reduce_sum | solution.py:52
  652.0 49.8 %fusion.17 = (bf16[2,3200,1024]{2,1,0:T(8,128)(2,1)}, f32[2,3200,1024]{2,1,0:T(8,128)}, f32[2,3200,1024]{2,1,0:T(8,128)}) fusion(bf16[2,3200,1024]{2,1,0:T(8,128)(2,1)} %param.15, f32[]{:T(128)S(6)} %min_shard_map.3, bf16[1,3200,1024]{2,1,0:T(8,128)(2,1)} %get-tuple-element.13, bf16[1,3200,1024]{2,1,0:T(8,128)(2,1)} %get-tuple-element.14, ...), kind=kLoop, calls=%fused_computation.32 | loop fusion | flops 131072000 | bytes 144179200 | tf_op jit(solution)/shard_map/convert_element_type | solution.py:30
  701.7 91.3 %fusion.8 = (bf16[2,1024,3200]{2,1,0:T(8,128)(2,1)}, f32[2,1024,3200]{2,1,0:T(8,128)}, f32[2,1024,3200]{2,1,0:T(8,128)}, bf16[2,1024,3200]{2,1,0:T(8,128)(2,1)},...) fusion(bf16[2,1024,3200]{2,1,0:T(8,128)(2,1)} %param.13, f32[]{:T(128)S(6)} %min_shard_map.3, ...), kind=kLoop, calls=%fused_computation.23 | loop fusion | flops 262144000 | bytes 288358400 | tf_op jit(solution)/shard_map/convert_element_type | solution.py:30
  (48 shorter events, 2.0 us)
Async XLA Ops:
  7.2 606.4 %all-reduce.3.cloned.1.call-start = ((), (), s32[]{:S(2)}) async-start(), calls=%async_computation | async-start | bytes 78643200 | tf_op jit(solution)/shard_map/psum | solution.py:50
  10.1 44.5 %copy-start.1 = (bf16[1,1024,1024]{1,2,0:T(8,128)(2,1)}, bf16[1,1024,1024]{1,2,0:T(8,128)(2,1)S(1)}, u32[]{:S(2)}) copy-start(bf16[1,1024,1024]{1,2,0:T(8,128)(2,1)S(1)} %copy.20) | copy-start | bytes 6291460
  10.6 27.2 %copy-start.9 = (f32[1024]{0:T(1024)}, f32[1024]{0:T(1024)S(1)}, u32[]{:S(2)}) copy-start(f32[1024]{0:T(1024)S(1)} %add_rsqrt_fusion) | copy-start | bytes 12292
  10.6 16.7 %slice-start.4 = ((s8[13107200]{0:T(1024)(128)(4,1)}), s8[524288]{0:T(1024)(128)(4,1)S(1)}, s32[]{:S(2)}) async-start(s8[13107200]{0:T(1024)(128)(4,1)} %bitcast.76), calls=%async_computation.5 | async-start | bytes 1048576
  14.8 12.5 %slice-start.5 = ((s8[13107200]{0:T(1024)(128)(4,1)}), s8[4194304]{0:T(1024)(128)(4,1)S(1)}, s32[]{:S(2)}) async-start(s8[13107200]{0:T(1024)(128)(4,1)} %bitcast.76), calls=%async_computation.6 | async-start | bytes 8388608
  14.8 12.5 %slice-start.6 = ((s8[13107200]{0:T(1024)(128)(4,1)}), s8[4194304]{0:T(1024)(128)(4,1)S(1)}, s32[]{:S(2)}) async-start(s8[13107200]{0:T(1024)(128)(4,1)} %bitcast.76), calls=%async_computation.7 | async-start | bytes 8388608
  14.8 12.5 %slice-start.7 = ((s8[13107200]{0:T(1024)(128)(4,1)}), s8[4194304]{0:T(1024)(128)(4,1)S(1)}, s32[]{:S(2)}) async-start(s8[13107200]{0:T(1024)(128)(4,1)} %bitcast.76), calls=%async_computation.8 | async-start | bytes 8388608
  14.8 12.5 %copy-start.5 = (bf16[1,1024,1024]{2,1,0:T(8,128)(2,1)S(1)}, bf16[1,1024,1024]{2,1,0:T(8,128)(2,1)}, u32[]{:S(2)}) copy-start(bf16[1,1024,1024]{2,1,0:T(8,128)(2,1)} %param.11) | copy-start | bytes 6291460
  66.2 1.3 copy-start.3
  66.2 38.0 %copy-start.7 = (f32[1024]{0:T(1024)}, f32[1024]{0:T(1024)S(1)}, u32[]{:S(2)}) copy-start(f32[1024]{0:T(1024)S(1)} %get-tuple-element.26) | copy-start | bytes 12292
  104.2 13.5 %copy-start.4 = (bf16[1024,1024]{0,1:T(8,128)(2,1)S(1)}, bf16[1024,1024]{0,1:T(8,128)(2,1)}, u32[]{:S(2)}) copy-start(bf16[1024,1024]{0,1:T(8,128)(2,1)} %copy-done.3) | copy-start | bytes 6291460
  117.7 14.7 %copy-start.6 = (bf16[1,1024,1024]{2,1,0:T(8,128)(2,1)S(1)}, bf16[1,1024,1024]{2,1,0:T(8,128)(2,1)}, u32[]{:S(2)}) copy-start(bf16[1,1024,1024]{2,1,0:T(8,128)(2,1)} %param.12) | copy-start | bytes 6291460
  147.1 25.5 %slice-start = ((s8[13107200]{0:T(1024)(128)(4,1)}), s8[4194304]{0:T(1024)(128)(4,1)S(1)}, s32[]{:S(2)}) async-start(s8[13107200]{0:T(1024)(128)(4,1)} %bitcast.74), calls=%async_computation.1 | async-start | bytes 8388608
  147.1 25.5 %slice-start.1 = ((s8[13107200]{0:T(1024)(128)(4,1)}), s8[4194304]{0:T(1024)(128)(4,1)S(1)}, s32[]{:S(2)}) async-start(s8[13107200]{0:T(1024)(128)(4,1)} %bitcast.74), calls=%async_computation.2 | async-start | bytes 8388608
  147.1 25.6 %slice-start.2 = ((s8[13107200]{0:T(1024)(128)(4,1)}), s8[4194304]{0:T(1024)(128)(4,1)S(1)}, s32[]{:S(2)}) async-start(s8[13107200]{0:T(1024)(128)(4,1)} %bitcast.74), calls=%async_computation.3 | async-start | bytes 8388608
  159.1 11.9 %copy-start.8 = (f32[1024]{0:T(1024)S(1)}, f32[1024]{0:T(1024)}, u32[]{:S(2)}) copy-start(f32[1024]{0:T(1024)} %copy-done.7) | copy-start | bytes 12292
  159.1 11.9 %copy-start = (bf16[1,1024,1024]{1,2,0:T(8,128)(2,1)S(1)}, bf16[1,1024,1024]{1,2,0:T(8,128)(2,1)}, u32[]{:S(2)}) copy-start(bf16[1,1024,1024]{1,2,0:T(8,128)(2,1)} %copy.21) | copy-start | bytes 6291460
  159.1 13.5 %slice-start.3 = ((s8[13107200]{0:T(1024)(128)(4,1)}), s8[524288]{0:T(1024)(128)(4,1)S(1)}, s32[]{:S(2)}) async-start(s8[13107200]{0:T(1024)(128)(4,1)} %bitcast.74), calls=%async_computation.4 | async-start | bytes 1048576
  182.0 12.0 %copy-start.2 = (bf16[1,1024,1024]{1,2,0:T(8,128)(2,1)S(1)}, bf16[1,1024,1024]{1,2,0:T(8,128)(2,1)}, u32[]{:S(2)}) copy-start(bf16[1,1024,1024]{1,2,0:T(8,128)(2,1)} %copy-done.1) | copy-start | bytes 6291460
  182.0 12.0 %copy-start.10 = (f32[1024]{0:T(1024)S(1)}, f32[1024]{0:T(1024)}, u32[]{:S(2)}) copy-start(f32[1024]{0:T(1024)} %copy-done.9) | copy-start | bytes 12292
  182.0 12.0 %copy-start.11 = (bf16[1024,3200]{1,0:T(8,128)(2,1)S(1)}, bf16[1024,3200]{1,0:T(8,128)(2,1)}, u32[]{:S(2)}) copy-start(bf16[1024,3200]{1,0:T(8,128)(2,1)} %convolution_convert_fusion.3) | copy-start | bytes 19660804
Sparse Core Ops, SparseCore 0:
  224.4 389.1 all-reduce.2
where the time goes:
time: 808 us; the launch traced here: 800 us
  waiting for transfers between devices  389 us (48%)
  matrix products  206 us (25%)
  other arithmetic  180 us (22%)
  between operations  16.5 us (2%)
  local copies, waits for them, and re-layouts  8.42 us (1%)
    psum x1, waiting for transfers between devices, step(): summed[number] = [lax.psum(by_w[name], 'dp') for name in NAMES]  389 us
    convert_element_type x2, other arithmetic, adamw(): return ((w - 0.02 * step).astype(jnp.bfloat16), m, v)  141 us
    dot_general x5, matrix products, layer(): gate = jnp.dot(a, w['w_gate'], preferred_element_type=jnp.float32)  74.7 us
    dot_general x5, matrix products, layer(): up = jnp.dot(a, w['w_up'], preferred_element_type=jnp.float32)  71.4 us
    dot_general x5, matrix products, matmul(): jnp.dot(a, w, preferred_element_type=jnp.float32).astype(jnp.bfloat16)  60.2 us
    reduce_sum x3, other arithmetic, step(): jnp.sum(g * g)  36.4 us
  transfers between devices with their start and end apart: 1, of which 1 were waited for; matrix products, arithmetic and copies ran while one was open for 0% of the time, Pallas kernels for 0%

commit v1 on v0

v1 whole, which is shorter than its diff:
```python
import functools

import jax
import jax.numpy as jnp
from jax import lax
from jax.experimental import pallas as pl
from jax.experimental.pallas import tpu as pltpu
from jax.sharding import PartitionSpec as P

NAMES = ("w_gate", "w_up", "w_down")
SLOTS = 4


def matmul(a, w):
    return jnp.dot(a, w, preferred_element_type=jnp.float32).astype(jnp.bfloat16)


def normed(h):
    wide = h.astype(jnp.float32)
    scale = lax.rsqrt(jnp.mean(wide**2, -1, keepdims=True) + 1e-6)
    return (wide * scale).astype(jnp.bfloat16)


def layer(h, w):
    a = normed(h)
    gate = jnp.dot(a, w["w_gate"], preferred_element_type=jnp.float32)
    up = jnp.dot(a, w["w_up"], preferred_element_type=jnp.float32)
    return h + matmul((jax.nn.silu(gate) * up).astype(jnp.bfloat16), w["w_down"])


MESH = pl.DeviceIdType.MESH
DEEP = 3
TILES = 5


def hops():
    me = lax.axis_index("dp")
    c, x = me % 2, me // 2
    a = x + 1 - 2 * (x % 2)
    return me, c, x, a, 3 - x, 3 - a


def backward_kernel(
    n, layers, x_ref, *refs
):
    inner, refs = refs[: layers - 1], refs[layers - 1 :]
    dy_ref, wg_ref, wu_ref, wd_ref, refs = *refs[:4], refs[4:]
    gu_outs, d_outs, factor_ref, refs = refs[:layers], refs[layers : 2 * layers], refs[2 * layers], refs[2 * layers + 1 :]
    (h, a, aT, dh, dhT, wg, wu, wd, act, dgate, dup, acc_g, acc_u, send0, own, rcv0, rcv1, rcv2, fin, squares, parts,
     w_sem, h_sem, send0_sem, rcv0_sem, send1_sem, rcv1_sem, send2_sem, rcv2_sem, fin_sem, ssend_sem, srecv_sem,
     credit_p, credit_a, credit_b) = refs
    me, c, x, xa, xb, xo = hops()
    peer, to_a, to_b = 2 * x + 1 - c, 2 * xa + c, 2 * xb + c
    tokens, depth = h.shape
    width = wg.shape[-1]
    steps = layers * TILES
    half = depth // 2
    tall = 256
    inputs = (x_ref, *inner)

    def load_h(number):
        return pltpu.make_async_copy(inputs[number], h, h_sem.at[0])

    def weights_of(s):
        number, j, slot = layers - 1 - s // TILES, s % TILES, s % 2
        at = pl.ds(pl.multiple_of(j * width, width), width)
        return [
            pltpu.make_async_copy(wg_ref.at[number, :, at], wg.at[slot], w_sem.at[0, slot]),
            pltpu.make_async_copy(wu_ref.at[number, :, at], wu.at[slot], w_sem.at[1, slot]),
            pltpu.make_async_copy(wd_ref.at[number, at], wd.at[slot], w_sem.at[2, slot]),
        ]

    def turn(source, target):
        @pl.loop(0, tokens // 128)
        def _(r):
            at = pl.ds(pl.multiple_of(r * 128, 128), 128)
            target[:, at] = source[at, :].T

    def norm():
        @pl.loop(0, tokens // 64)
        def _(r):
            at = pl.ds(pl.multiple_of(r * 64, 64), 64)
            wide = h[at].astype(jnp.float32)
            scale = lax.rsqrt(jnp.mean(wide**2, -1, keepdims=True) + 1e-6)
            a[at] = (wide * scale).astype(jnp.bfloat16)

    load_h(layers - 1).start()
    first_dh = pltpu.make_async_copy(dy_ref, dh, h_sem.at[1])
    first_dh.start()
    for one in weights_of(0):
        one.start()

    barrier = pltpu.get_barrier_semaphore()
    for k in range(1, n):
        pl.semaphore_signal(barrier, inc=1, device_id={"dp": (me + k) % n}, device_id_type=MESH)
    pl.semaphore_wait(barrier, n - 1)

    load_h(layers - 1).wait()
    norm()
    turn(a, aT)
    first_dh.wait()
    turn(dh, dhT)

    def remote(source, target, sends, receives, to):
        return pltpu.make_async_remote_copy(
            src_ref=source, dst_ref=target, send_sem=sends, recv_sem=receives, device_id={"dp": to}, device_id_type=MESH
        )

    def swap(s):
        return remote(send0.at[s % 2], rcv0.at[s % DEEP], send0_sem.at[s % 2], rcv0_sem.at[s % DEEP], peer)

    def step_one(s):
        k = s % DEEP
        blocks = ((2 * xa, to_a), (2 * xo, to_a), (2 * xb + 1, to_b), (2 * xo + 1, to_b))
        return [(b, remote(own.at[k, b], rcv1.at[k, i], send1_sem.at[k, i], rcv1_sem.at[k, i], to)) for i, (b, to) in enumerate(blocks)]

    def step_two(s):
        k = s % DEEP
        blocks = ((2 * xb, to_b, 1), (2 * xa + 1, to_a, 3))
        return [
            (b, got, remote(own.at[k, b], rcv2.at[k, i], send2_sem.at[k, i], rcv2_sem.at[k, i], to)) for i, (b, to, got) in enumerate(blocks)
        ]

    def summed(s, b, more):
        k = s % DEEP
        for mat in range(3):
            for r in range(0, own.shape[-2], 16):
                at = pl.ds(r, 16)
                total = own[k, b, mat, at].astype(jnp.float32) + rcv0[k, b, mat, at].astype(jnp.float32)
                for ref, i in more:
                    total = total + ref[k, i, mat, at].astype(jnp.float32)
                yield mat, at, total.astype(jnp.bfloat16)

    def begin(s):
        swap(s).wait_recv()

        @pl.when(s >= DEEP)
        def _():
            pl.semaphore_wait(credit_a, 1)
            pl.semaphore_wait(credit_b, 1)

        copies = step_one(s)
        for b, _ in copies:
            for mat, at, total in summed(s, b, ()):
                own[s % DEEP, b, mat, at] = total
        for _, one in copies:
            one.start()

    def pass_on(s):
        for _, one in step_one(s):
            one.wait_recv()
        copies = step_two(s)
        for b, got, _ in copies:
            for mat, at, total in summed(s, b, ((rcv1, got),)):
                own[s % DEEP, b, mat, at] = total
        for *_, one in copies:
            one.start()

    def fin_copies(s, number):
        at = pl.ds(pl.multiple_of((s % TILES) * width, width), width)
        return [
            pltpu.make_async_copy(fin.at[:, 0:2], gu_outs[number].at[:, :, :, at], fin_sem.at[0]),
            pltpu.make_async_copy(fin.at[:, 2], d_outs[number].at[:, :, at], fin_sem.at[1]),
        ]

    def finish(s):
        for *_, one in step_two(s):
            one.wait_recv()

        @pl.when(s >= 1)
        def _():
            for one in fin_copies(s, 0):
                one.wait()

        for colour in range(2):
            for mat, at, total in summed(s, 2 * x + colour, ((rcv1, 2 * colour), (rcv2, colour))):
                fin[colour, mat, at] = total
                squared = total.astype(jnp.float32) ** 2
                squares[...] += squared[:8] + squared[8:]
        for number in range(layers):

            @pl.when(layers - 1 - s // TILES == number)
            def _():
                for one in fin_copies(s, number):
                    one.start()

        for _, one in step_one(s):
            one.wait_send()
        for *_, one in step_two(s):
            one.wait_send()

        @pl.when(s + DEEP < steps)
        def _():
            pl.semaphore_signal(credit_p, inc=1, device_id={"dp": peer}, device_id_type=MESH)
            pl.semaphore_signal(credit_a, inc=1, device_id={"dp": to_a}, device_id_type=MESH)
            pl.semaphore_signal(credit_b, inc=1, device_id={"dp": to_b}, device_id_type=MESH)

    def gradients(core, keep):
        for_rows = half // tall

        @pl.loop(0, for_rows)
        def _(r):
            at = pl.ds(pl.multiple_of(core * half + r * tall, tall), tall)
            blocks = tall // 64
            for mat, (left, right) in enumerate(((aT, dgate), (aT, dup), (dhT, act))):
                got = jnp.dot(left[at], right[...], preferred_element_type=jnp.float32).astype(jnp.bfloat16)
                for b in range(blocks):
                    keep(r * blocks + b, mat, got[b * 64 : (b + 1) * 64])

    squares[...] = jnp.zeros_like(squares)

    @pl.loop(0, steps)
    def _(s):
        slot, k = s % 2, s % DEEP
        for one in weights_of(s):
            one.wait()

        @pl.when(s + 1 < steps)
        def _():
            for one in weights_of(s + 1):
                one.start()

        @pl.loop(0, tokens // tall)
        def _(r):
            at = pl.ds(pl.multiple_of(r * tall, tall), tall)
            gate = jnp.dot(a[at], wg[slot], preferred_element_type=jnp.float32)
            up = jnp.dot(a[at], wu[slot], preferred_element_type=jnp.float32)
            by_act = lax.dot_general(dh[at], wd[slot], (((1,), (1,)), ((), ())), preferred_element_type=jnp.float32)
            by_act = by_act.astype(jnp.bfloat16).astype(jnp.float32)
            share = jax.nn.sigmoid(gate)
            silu = gate * share
            act[at] = (silu * up).astype(jnp.bfloat16)
            dup[at] = (by_act * silu).astype(jnp.bfloat16)
            dgate[at] = (by_act * up * (share + silu * (1.0 - share))).astype(jnp.bfloat16)

        @pl.when(s >= 2)
        def _():
            swap(s).wait_send()

        def to_send(b, mat, value):
            send0[slot, b, mat] = value

        gradients(1 - c, to_send)

        @pl.when(s >= DEEP)
        def _():
            pl.semaphore_wait(credit_p, 1)

        swap(s).start()

        def to_own(b, mat, value):
            own[k, b, mat] = value

        gradients(c, to_own)
        begin(s)

        @pl.when(s >= 1)
        def _():
            pass_on(s - 1)

        @pl.when(s >= 2)
        def _():
            finish(s - 2)

        @pl.when(s < steps - TILES)
        def _():
            @pl.when(s % TILES == 0)
            def _():
                acc_g[...] = jnp.zeros_like(acc_g)
                acc_u[...] = jnp.zeros_like(acc_u)

            @pl.loop(0, tokens // tall)
            def _(r):
                at = pl.ds(pl.multiple_of(r * tall, tall), tall)
                for total, by, w in ((acc_g, dgate, wg), (acc_u, dup, wu)):
                    total[at] += lax.dot_general(by[at], w[slot], (((1,), (1,)), ((), ())), preferred_element_type=jnp.float32)

            @pl.when(s % TILES == TILES - 1)
            def _():
                @pl.loop(0, tokens // 32)
                def _(r):
                    at = pl.ds(pl.multiple_of(r * 32, 32), 32)
                    by = acc_g[at].astype(jnp.bfloat16) + acc_u[at].astype(jnp.bfloat16)
                    by, wide = by.astype(jnp.float32), h[at].astype(jnp.float32)
                    scale = lax.rsqrt(jnp.mean(wide**2, -1, keepdims=True) + 1e-6)
                    inner = jnp.mean(by * wide, -1, keepdims=True)
                    by_h = (by * scale - wide * (scale * scale * scale * inner)).astype(jnp.bfloat16)
                    dh[at] = dh[at] + by_h

                for number in range(layers - 1):

                    @pl.when(layers - 2 - s // TILES == number)
                    def _():
                        load_h(number).start()
                        load_h(number).wait()

                norm()
                turn(a, aT)
                turn(dh, dhT)

    pass_on(jnp.int32(steps - 1))
    finish(jnp.int32(steps - 2))
    finish(jnp.int32(steps - 1))
    for one in fin_copies(jnp.int32(steps - 1), 0):
        one.wait()
    swap(jnp.int32(steps - 2)).wait_send()
    swap(jnp.int32(steps - 1)).wait_send()

    parts[me] = sum(squares[:, k * 128 : (k + 1) * 128] for k in range(width // 128))

    def share(k):
        return remote(parts.at[me], parts.at[me], ssend_sem.at[k], srecv_sem.at[k], (me + k) % n)

    for k in range(1, n):
        share(k).start()
    for k in range(1, n):
        share(k).wait()
    total = parts[0]
    for k in range(1, n):
        total = total + parts[k]
    count = steps * width * depth * 3
    factor_ref[...] = jnp.minimum(1.0, 0.5 * lax.rsqrt(jnp.full(factor_ref.shape, jnp.sum(total)) / count + 1e-30))


def backward(n, inputs, dy, weights):
    layers, depth, hidden = weights[0].shape
    tokens, width, rows = dy.shape[0], hidden // TILES, depth // 16
    bf16, dma, regular = jnp.bfloat16, pltpu.SemaphoreType.DMA, pltpu.SemaphoreType.REGULAR
    any_spec = pl.BlockSpec(memory_space=pl.ANY)
    out = pl.pallas_call(
        functools.partial(backward_kernel, n, layers),
        out_shape=[jax.ShapeDtypeStruct((2, 2, rows, hidden), bf16)] * layers
        + [jax.ShapeDtypeStruct((2, rows, hidden), bf16)] * layers
        + [jax.ShapeDtypeStruct((8, 128), jnp.float32)],
        in_specs=[any_spec] * (layers + 4),
        out_specs=[any_spec] * (2 * layers) + [pl.BlockSpec(memory_space=pltpu.VMEM)],
        scratch_shapes=[
            pltpu.VMEM((tokens, depth), bf16),
            pltpu.VMEM((tokens, depth), bf16),
            pltpu.VMEM((depth, tokens), bf16),
            pltpu.VMEM((tokens, depth), bf16),
            pltpu.VMEM((depth, tokens), bf16),
            pltpu.VMEM((2, depth, width), bf16),
            pltpu.VMEM((2, depth, width), bf16),
            pltpu.VMEM((2, width, depth), bf16),
            pltpu.VMEM((tokens, width), bf16),
            pltpu.VMEM((tokens, width), bf16),
            pltpu.VMEM((tokens, width), bf16),
            pltpu.VMEM((tokens, depth), jnp.float32),
            pltpu.VMEM((tokens, depth), jnp.float32),
            pltpu.VMEM((2, 8, 3, rows, width), bf16),
            pltpu.VMEM((DEEP, 8, 3, rows, width), bf16),
            pltpu.VMEM((DEEP, 8, 3, rows, width), bf16),
            pltpu.VMEM((DEEP, 4, 3, rows, width), bf16),
            pltpu.VMEM((DEEP, 2, 3, rows, width), bf16),
            pltpu.VMEM((2, 3, rows, width), bf16),
            pltpu.VMEM((8, width), jnp.float32),
            pltpu.VMEM((n, 8, 128), jnp.float32),
            dma((3, 2)),
            dma((2,)),
            dma((2,)),
            dma((DEEP,)),
            dma((DEEP, 4)),
            dma((DEEP, 4)),
            dma((DEEP, 2)),
            dma((DEEP, 2)),
            dma((2,)),
            dma((n,)),
            dma((n,)),
            regular,
            regular,
            regular,
        ],
        compiler_params=pltpu.CompilerParams(collective_id=0, has_side_effects=True, vmem_limit_bytes=67_043_328),
        cost_estimate=pl.CostEstimate(flops=16 * tokens * depth * hidden * layers, bytes_accessed=2**27, transcendentals=0),
    )(*inputs, dy, *weights)
    return out[:layers], out[layers : 2 * layers], out[-1]


def update_kernel(items, n_new, *refs):
    n_g = 1 + max(item[0] for item in items)
    factor_ref, refs = refs[0], refs[1:]
    g_refs, refs = refs[:n_g], refs[n_g:]
    old, refs = refs[:9], refs[9:]
    if not n_new:
        refs = refs[9:]
    new, refs = refs[:9], refs[9:]
    factor_vmem, wide, tall, in_sem, out_sem, f_sem = refs
    c, x = place()
    copy = pltpu.make_async_copy(factor_ref, factor_vmem, f_sem)
    copy.start()
    copy.wait()
    factor = factor_vmem[0:1, 0:1]

    def views(n):
        which, tile, weight, layer, core, rel, colour = items[n]
        slot = n % SLOTS
        buffers = [b.at[slot] for b in (tall if weight == 2 else wide)]
        rows, cols = buffers[0].shape
        owner = spot(c, x, core, rel)
        if weight == 2:
            index = (layer, pl.ds(colour * rows, rows), pl.ds(pl.multiple_of(owner * cols, cols), cols))
        else:
            index = (layer, pl.ds(pl.multiple_of((owner * 2 + colour) * rows, rows), rows))
        sources = [old[3 * j + weight].at[index] for j in range(3)] + [g_refs[which].at[tile]]
        targets = [new[3 * j + weight].at[index] for j in range(3)]
        return buffers, sources, targets, slot

    def loads(n):
        buffers, sources, _, slot = views(n)
        return [pltpu.make_async_copy(s, b, in_sem.at[j, slot]) for j, (s, b) in enumerate(zip(sources, buffers, strict=True))]

    def stores(n):
        buffers, _, targets, slot = views(n)
        return [pltpu.make_async_copy(b, t, out_sem.at[j, slot]) for j, (b, t) in enumerate(zip(buffers[:3], targets, strict=True))]

    ahead = SLOTS - 2
    for n in range(min(ahead, len(items))):
        for one in loads(n):
            one.start()
    for n in range(len(items)):
        if n + ahead < len(items):
            if n + ahead - SLOTS >= 0:
                for one in stores(n + ahead - SLOTS):
                    one.wait()
            for one in loads(n + ahead):
                one.start()
        for one in loads(n):
            one.wait()
        w_ref, m_ref, v_ref, g_ref = views(n)[0]
        rows, cols = w_ref.shape
        across = cols // 5 if cols % 5 == 0 else cols

        @pl.loop(0, rows // 16)
        def _(r):
            at = pl.ds(pl.multiple_of(r * 16, 16), 16)
            for k in range(cols // across):
                lanes = pl.ds(k * across, across)
                g = g_ref[at, lanes].astype(jnp.float32) * factor
                m = 0.9 * m_ref[at, lanes] + 0.1 * g
                v = 0.95 * v_ref[at, lanes] + 0.05 * g * g
                w = w_ref[at, lanes].astype(jnp.float32)
                move = m * lax.rsqrt(v + 1e-8) + 0.1 * w
                w_ref[at, lanes] = (w - 0.02 * move).astype(jnp.bfloat16)
                m_ref[at, lanes] = m
                v_ref[at, lanes] = v

        for one in stores(n):
            one.start()
    for n in range(max(0, len(items) - SLOTS), len(items)):
        for one in stores(n):
            one.wait()


def place():
    me = lax.axis_index("dp")
    return me % 2, me // 2


def spot(c, x, core, rel):
    near = x + (rel % 2) * (1 - 2 * (x % 2))
    return (c + core) % 2 * 4 + (3 - near if rel // 2 else near)


def update(factor, items, gs, old, new):
    rows, cols = old[0].shape[1:]
    down_rows, down_cols = old[2].shape[1:]
    wide, tall = (rows // 16, cols), (down_rows // 2, down_cols // 8)

    def slots(shape):
        return [pltpu.VMEM((SLOTS, *shape), t) for t in (jnp.bfloat16, jnp.float32, jnp.float32, jnp.bfloat16)]

    any_spec = pl.BlockSpec(memory_space=pl.ANY)
    n_in = 1 + len(gs) + 9 + (9 if new is not None else 0)
    size = len(items) * wide[0] * wide[1]
    return pl.pallas_call(
        functools.partial(update_kernel, items, new is None),
        out_shape=[jax.ShapeDtypeStruct(o.shape, o.dtype) for o in old],
        in_specs=[any_spec] * n_in,
        out_specs=[any_spec] * 9,
        scratch_shapes=[
            pltpu.VMEM((8, 128), jnp.float32),
            slots(wide),
            slots(tall),
            pltpu.SemaphoreType.DMA((4, SLOTS)),
            pltpu.SemaphoreType.DMA((3, SLOTS)),
            pltpu.SemaphoreType.DMA,
        ],
        input_output_aliases={} if new is None else {n_in - 9 + i: i for i in range(9)},
        cost_estimate=pl.CostEstimate(flops=size * 400, bytes_accessed=size * 22, transcendentals=size),
        compiler_params=pltpu.CompilerParams(vmem_limit_bytes=32 * 2**20),
    )(factor, *gs, *old, *(new if new is not None else ()))


def solution(mesh):
    n = mesh.shape["dp"]
    chips = n // 2
    pair_a = [(2 * x + c, 2 * (x ^ 1) + c) for x in range(chips) for c in range(2)]
    pair_b = [(2 * x + c, 2 * (chips - 1 - x) + c) for x in range(chips) for c in range(2)]
    peers = [(i, i ^ 1) for i in range(n)]
    to_a, to_b, to_peer = (functools.partial(lax.ppermute, axis_name="dp", perm=perm) for perm in (pair_a, pair_b, peers))

    def step(x, dy, *arrays):
        weights = arrays[:3]
        layers = weights[0].shape[0]
        h, kept = x[0], []
        for number in range(layers):
            kept.append(h)
            if number < layers - 1:
                h = layer(h, {name: w[number] for name, w in zip(NAMES, weights, strict=True)})
        wide, tall, factor = backward(n, kept, dy[0], weights)
        shards = []
        for number in reversed(range(layers)):
            down = tall[number].reshape(-1, tall[number].shape[-1]).T
            shards.append((number, 2, down.reshape(2, 1, down.shape[0] // 2, down.shape[1])))
            shards.append((number, 0, wide[number]))

        def run(new, parts):
            items, gs = [], []
            for unit, g, core, rel, colour in parts:
                number, weight, own = shards[unit]
                for this in range(2) if colour is None else (colour,):
                    for kind in range(own.shape[1]):
                        tile = (this, kind) if colour is None else (kind,)
                        items.append((len(gs), tile, weight + kind, number, core, rel, this))
                gs.append(g)
            return update(factor, items, gs, arrays, new)

        def after(new, waited):
            first, waited = lax.optimization_barrier((new[0], waited))
            return [first, *new[1:]], waited

        owns = [own for _, _, own in shards]
        near = [(to_a(own), to_b(own)) for own in owns]
        beside = [to_peer(own) for own in owns]
        new = run(None, [(u, own, 0, 0, None) for u, own in enumerate(owns)] + [(u, g, 1, 0, None) for u, g in enumerate(beside)])
        groups, far = [(0, 1), (2, 3)], []
        for i, group in enumerate(groups):
            new, got = after(new, [near[u] for u in group])
            far.append([(to_a(from_b[0]), to_b(from_a[1])) for from_a, from_b in got])
            beside = [(to_peer(from_a), to_peer(from_b)) for from_a, from_b in got]
            new = run(new, [(u, g, 0, 1 + j, None) for u, pair in zip(group, got, strict=True) for j, g in enumerate(pair)])
            new = run(new, [(u, g, 1, 1 + j, None) for u, pair in zip(group, beside, strict=True) for j, g in enumerate(pair)])
        for i, group in enumerate(groups):
            new, got = after(new, far[i])
            beside = [(to_peer(over_a), to_peer(over_b)) for over_a, over_b in got]
            new = run(new, [(u, g, 0, 3, j) for u, pair in zip(group, got, strict=True) for j, g in enumerate(pair)])
            new = run(new, [(u, g, 1, 3, j) for u, pair in zip(group, beside, strict=True) for j, g in enumerate(pair)])
        return tuple(new)

    return jax.shard_map(
        step,
        mesh=mesh,
        in_specs=(P(("rep", "dp"), None, None),) * 2 + (P(None, None, None),) * 9,
        out_specs=(P("rep", None, None),) * 9,
        check_vma=False,
    )
```

time: 808 us -> 505 us (0.62)
  Pallas kernels: 0 us -> 419 us
  waiting for transfers between devices: 389 us -> 2.91 us
  other arithmetic: 180 us -> 2.07 us
  matrix products: 206 us -> 36.1 us
  starting transfers between devices: 0.06 us -> 23.4 us
  between operations: 16.5 us -> 1.16 us
  local copies, waits for them, and re-layouts: 8.42 us -> 19.5 us
    pallas_call x0 -> x10, Pallas kernels: none -> 419 us  [the longest x1 211 us: backward(): pl.pallas_call(functools.partial(backward_kernel, n, layers), out_shape=[...]
    psum x1 -> x0, waiting for transfers between devices: 389 us -> none  [step(): summed[number] = [lax.psum(by_w[name], 'dp') for name in NAMES]]
    convert_element_type x2 -> x0, other arithmetic: 141 us -> none  [adamw(): return ((w - 0.02 * step).astype(jnp.bfloat16), m, v)]
    dot_general x5 -> x0, matrix products: 71.4 us -> none  [layer(): up = jnp.dot(a, w['w_up'], preferred_element_type=jnp.float32)]
    dot_general x5 -> x1, matrix products: 74.7 us -> 13.7 us  [layer(): gate = jnp.dot(a, w['w_gate'], preferred_element_type=jnp.float32)]
    dot_general x5 -> x1, matrix products: 60.2 us -> 22.3 us  [matmul(): jnp.dot(a, w, preferred_element_type=jnp.float32).astype(jnp.bfloat16)]
    reduce_sum x3 -> x0, other arithmetic: 36.4 us -> none  [step(): jnp.sum(g * g)]
    ppermute x0 -> x36, starting transfers between devices: none -> 23.4 us  [the longest x8 9.78 us: step(): far.append([(to_a(from_b[0]), to_b(from_a[1])) for from_a, from_b in got])]
  transfers between devices with their start and end apart: 1 -> 36, of which waited for: 1 -> 3; matrix products, arithmetic and copies ran while one was open for 0% -> 3% of each run, Pallas kernels for 0% -> 38%
where the time goes in v1:
time: 505 us; the launch traced here: 504 us
  Pallas kernels  419 us (83%)
  matrix products  36.1 us (7%)
  starting transfers between devices  23.4 us (5%)
  local copies, waits for them, and re-layouts  19.5 us (4%)
    pallas_call x1, Pallas kernels, backward(): pl.pallas_call(functools.partial(backward_kernel, n, layers), out_shape=[...  211 us
    pallas_call x9, Pallas kernels, update(): pl.pallas_call(functools.partial(update_kernel, items, new is None), out_...  207 us
    dot_general x1, matrix products, matmul(): jnp.dot(a, w, preferred_element_type=jnp.float32).astype(jnp.bfloat16)  22.3 us
    dot_general x1, matrix products, layer(): gate = jnp.dot(a, w['w_gate'], preferred_element_type=jnp.float32)  13.7 us
  transfers between devices with their start and end apart: 36, of which 3 were waited for; matrix products, arithmetic and copies ran while one was open for 3% of the time, Pallas kernels for 38%

profile of v1, /device:TPU:112, one launch (start us, length us, event | category | flops | bytes accessed | tf_op | source)
XLA Modules:
  0.0 503.7 jit_solution(2898117005459750821)
XLA Ops:
  0.6 2.1 multiply_reduce_fusion
  2.7 13.7 %fusion.4 = f32[1024,3200]{1,0:T(8,128)} fusion(bf16[2,1024,3200]{2,1,0:T(8,128)(2,1)} %refs_5_.15, bf16[1,1024,1024]{2,1,0:T(8,128)(2,1)} %param.11, f32[1024]{0:T(1024)S(1)} %add_rsqrt_fusion), kind=kOutput, calls=%fused_computation.4 | convolution fusion | flops 6714032128 | bytes 21762048 | tf_op jit(solution)/shard_map/dot_general | solution.py:26
  16.5 22.3 %convert_add_fusion.refs_0_ = bf16[1024,1024]{1,0:T(8,128)(2,1)} fusion(bf16[2,3200,1024]{2,1,0:T(8,128)(2,1)} %refs_7_.15, f32[1024,3200]{1,0:T(8,128)} %fusion.4, bf16[2,1024,3200]{2,1,0:T(8,128)(2,1)} %refs_6_.15, bf16[1,1024,1024]{2,1,0:T(8,128)(2,1)S(1)} %copy-done.4, f32[1024]{0:T(1024)S(1)} %add_rsqrt_fusion), kind=kOutput, calls=%fused_computation.13 | convolution fusion | flops 13449822208 | bytes 32509952 | tf_op jit(solution)/shard_map/dot_general | solution.py:15
  38.8 211.3 %shard_map.178 = (bf16[2,2,64,3200]{3,2,1,0:T(8,128)(2,1)}, bf16[2,2,64,3200]{3,2,1,0:T(8,128)(2,1)}, bf16[2,64,3200]{2,1,0:T(8,128)(2,1)}, bf16[2,64,3200]{2,1,0:T(8,128)(2,1)}, f32[8,128]{1,0:T(8,128)}) custom-call(bf16[1024,1024]{1,0:T(8,128)(2,1)} %bitcast.55, bf16[1024,1024]{1,0:T(8,128)(2,1)} %convert_add_fusion.refs_0_, bf16[1024,1024]{1,0:T(8,128)(2,1)} %bitcast.58, ...), custom_call_target="tpu_custom_call" | custom-call | flops 107374182400 | bytes 134217728 | tf_op jit(solution)/shard_map/pallas_call | solution.py:330
  250.3 1.7 copy.93
  252.6 1.7 copy.92
  254.8 1.6 collective-permute-start.7
  256.8 1.6 collective-permute-done.refs_5_
  258.4 1.6 collective-permute-start.5
  260.4 4.7 copy-done
  267.2 45.2 %shard_map.179 = (bf16[2,1024,3200]{2,1,0:T(8,128)(2,1)}, bf16[2,1024,3200]{2,1,0:T(8,128)(2,1)}, bf16[2,3200,1024]{2,1,0:T(8,128)(2,1)}, f32[2,1024,3200]{2,1,0...) custom-call(f32[8,128]{1,0:T(8,128)S(1)} %copy-done.2, ...), custom_call_target="tpu_custom_call" | custom-call | flops 1966080000 | bytes 108134400 | tf_op jit(solution)/shard_map/pallas_call | solution.py:476
  315.8 25.1 %shard_map.180 = (bf16[2,1024,3200]{2,1,0:T(8,128)(2,1)}, bf16[2,1024,3200]{2,1,0:T(8,128)(2,1)}, bf16[2,3200,1024]{2,1,0:T(8,128)(2,1)}, f32[2,1024,3200]{2,1,0...) custom-call(f32[8,128]{1,0:T(8,128)S(1)} %copy-done.3, ...), custom_call_target="tpu_custom_call", output_to_operand_aliasing={{0}: (14, {}), {1}: (15, {}), {2}: (16, {}), {3}: (17, {}),... | custom-call | flops 983040000 | bytes 54067200 | tf_op jit(solution)/shard_map/pallas_call | solution.py:476
  345.4 25.1 %shard_map.181 = (bf16[2,1024,3200]{2,1,0:T(8,128)(2,1)}, bf16[2,1024,3200]{2,1,0:T(8,128)(2,1)}, bf16[2,3200,1024]{2,1,0:T(8,128)(2,1)}, f32[2,1024,3200]{2,1,0...) custom-call(f32[8,128]{1,0:T(8,128)S(1)} %copy-done.3, ...), custom_call_target="tpu_custom_call", output_to_operand_aliasing={{0}: (14, {}), {1}: (15, {}), {2}: (16, {}), {3}: (17, {}),... | custom-call | flops 983040000 | bytes 54067200 | tf_op jit(solution)/shard_map/pallas_call | solution.py:476
  371.4 1.7 collective-permute-start.20
  374.6 2.1 slice_bitcast_fusion
  378.3 1.7 collective-permute-start.23
  380.0 2.1 slice_bitcast_fusion.1
  382.1 25.3 %shard_map.182 = (bf16[2,1024,3200]{2,1,0:T(8,128)(2,1)}, bf16[2,1024,3200]{2,1,0:T(8,128)(2,1)}, bf16[2,3200,1024]{2,1,0:T(8,128)(2,1)}, f32[2,1024,3200]{2,1,0...) custom-call(f32[8,128]{1,0:T(8,128)S(1)} %copy-done.3, ...), custom_call_target="tpu_custom_call", output_to_operand_aliasing={{0}: (14, {}), {1}: (15, {}), {2}: (16, {}), {3}: (17, {}),... | custom-call | flops 983040000 | bytes 54067200 | tf_op jit(solution)/shard_map/pallas_call | solution.py:476
  408.8 25.1 %shard_map.183 = (bf16[2,1024,3200]{2,1,0:T(8,128)(2,1)}, bf16[2,1024,3200]{2,1,0:T(8,128)(2,1)}, bf16[2,3200,1024]{2,1,0:T(8,128)(2,1)}, f32[2,1024,3200]{2,1,0...) custom-call(f32[8,128]{1,0:T(8,128)S(1)} %copy-done.3, ...), custom_call_target="tpu_custom_call", output_to_operand_aliasing={{0}: (14, {}), {1}: (15, {}), {2}: (16, {}), {3}: (17, {}),... | custom-call | flops 983040000 | bytes 54067200 | tf_op jit(solution)/shard_map/pallas_call | solution.py:476
  433.9 1.7 collective-permute-start.31
  440.9 15.3 %shard_map.184 = (bf16[2,1024,3200]{2,1,0:T(8,128)(2,1)}, bf16[2,1024,3200]{2,1,0:T(8,128)(2,1)}, bf16[2,3200,1024]{2,1,0:T(8,128)(2,1)}, f32[2,1024,3200]{2,1,0...) custom-call(f32[8,128]{1,0:T(8,128)S(1)} %copy-done.3, ...), custom_call_target="tpu_custom_call", output_to_operand_aliasing={{0}: (14, {}), {1}: (15, {}), {2}: (16, {}), {3}: (17, {}),... | custom-call | flops 491520000 | bytes 27033600 | tf_op jit(solution)/shard_map/pallas_call | solution.py:476
  456.2 15.4 %shard_map.185 = (bf16[2,1024,3200]{2,1,0:T(8,128)(2,1)}, bf16[2,1024,3200]{2,1,0:T(8,128)(2,1)}, bf16[2,3200,1024]{2,1,0:T(8,128)(2,1)}, f32[2,1024,3200]{2,1,0...) custom-call(f32[8,128]{1,0:T(8,128)S(1)} %copy-done.3, ...), custom_call_target="tpu_custom_call", output_to_operand_aliasing={{0}: (14, {}), {1}: (15, {}), {2}: (16, {}), {3}: (17, {}),... | custom-call | flops 491520000 | bytes 27033600 | tf_op jit(solution)/shard_map/pallas_call | solution.py:476
  472.8 15.3 %shard_map.186 = (bf16[2,1024,3200]{2,1,0:T(8,128)(2,1)}, bf16[2,1024,3200]{2,1,0:T(8,128)(2,1)}, bf16[2,3200,1024]{2,1,0:T(8,128)(2,1)}, f32[2,1024,3200]{2,1,0...) custom-call(f32[8,128]{1,0:T(8,128)S(1)} %copy-done.3, ...), custom_call_target="tpu_custom_call", output_to_operand_aliasing={{0}: (14, {}), {1}: (15, {}), {2}: (16, {}), {3}: (17, {}),... | custom-call | flops 491520000 | bytes 27033600 | tf_op jit(solution)/shard_map/pallas_call | solution.py:476
  488.2 15.4 %shard_map.187 = (bf16[2,1024,3200]{2,1,0:T(8,128)(2,1)}, bf16[2,1024,3200]{2,1,0:T(8,128)(2,1)}, bf16[2,3200,1024]{2,1,0:T(8,128)(2,1)}, f32[2,1024,3200]{2,1,0...) custom-call(f32[8,128]{1,0:T(8,128)S(1)} %copy-done.3, ...), custom_call_target="tpu_custom_call", output_to_operand_aliasing={{0}: (14, {}), {1}: (15, {}), {2}: (16, {}), {3}: (17, {}),... | custom-call | flops 491520000 | bytes 27033600 | tf_op jit(solution)/shard_map/pallas_call | solution.py:476
  (82 shorter events, 23.6 us)
Async XLA Ops:
  254.8 57.7 %collective-permute-start.7 = (bf16[2,2,64,3200]{3,2,1,0:T(8,128)(2,1)}, bf16[2,2,64,3200]{3,2,1,0:T(8,128)(2,1)S(1)}, u32[]{:S(2)}, u32[]{:S(2)}) collective-permute-start(bf16[2,2,64,3200]{3,2,1,0:T(8,128)(2,1)} %get-tuple-element.108.refs_2_), channel_id=1, source_target_pairs={{0,6},{1,7},{2,4},{3,5},{4,2},{5,3},{6,0},{7,1},{8,14},{9,15},{10,... | collective-permute-start | bytes 4915208 | tf_op jit(solution)/shard_map/ppermute | solution.py:534
  256.4 56.1 %collective-permute-start.6 = (bf16[2,2,64,3200]{3,2,1,0:T(8,128)(2,1)}, bf16[2,2,64,3200]{3,2,1,0:T(8,128)(2,1)S(1)}, u32[]{:S(2)}, u32[]{:S(2)}) collective-permute-start(bf16[2,2,64,3200]{3,2,1,0:T(8,128)(2,1)} %get-tuple-element.108.refs_2_), channel_id=1, source_target_pairs={{0,2},{1,3},{2,0},{3,1},{4,6},{5,7},{6,4},{7,5},{8,10},{9,11},{10,... | collective-permute-start | bytes 4915208 | tf_op jit(solution)/shard_map/ppermute | solution.py:534
  258.4 54.1 %collective-permute-start.5 = (bf16[2,1,1600,128]{3,2,1,0:T(8,128)(2,1)S(1)}, bf16[2,1,1600,128]{3,2,1,0:T(8,128)(2,1)S(1)}, u32[]{:S(2)}, u32[]{:S(2)}) collective-permute-start(bf16[2,1,1600,128]{3,2,1,0:T(8,128)(2,1)S(1)} %bitcast.52), channel_id=1, source_target_pairs={{0,6},{1,7},{2,4},{3,5},{4,2},{5,3},{6,0},{7,1},{8,14},{9,15},{10,... | collective-permute-start | bytes 2457608 | tf_op jit(solution)/shard_map/ppermute | solution.py:534
  260.0 52.4 %collective-permute-start.4 = (bf16[2,1,1600,128]{3,2,1,0:T(8,128)(2,1)S(1)}, bf16[2,1,1600,128]{3,2,1,0:T(8,128)(2,1)S(1)}, u32[]{:S(2)}, u32[]{:S(2)}) collective-permute-start(bf16[2,1,1600,128]{3,2,1,0:T(8,128)(2,1)S(1)} %bitcast.53), channel_id=1, source_target_pairs={{0,2},{1,3},{2,0},{3,1},{4,6},{5,7},{6,4},{7,5},{8,10},{9,11},{10,... | collective-permute-start | bytes 2457608 | tf_op jit(solution)/shard_map/ppermute | solution.py:534
  312.5 28.4 %collective-permute-start.8 = (bf16[2,1,1600,128]{3,2,1,0:T(8,128)(2,1)S(1)}, bf16[2,1,1600,128]{3,2,1,0:T(8,128)(2,1)S(1)}, u32[]{:S(2)}, u32[]{:S(2)}) collective-permute-start(bf16[2,1,1600,128]{3,2,1,0:T(8,128)(2,1)S(1)} %collective-permute-done.4.refs_1_), channel_id=1, source_target_pairs={{0,1},{1,0},{2,3},{3,2},{4,5},{5,4},{6,7},{7,6},{8,9},{9,8},{10,11... | collective-permute-start | bytes 2457608 | tf_op jit(solution)/shard_map/ppermute | solution.py:541
  312.6 31.4 %collective-permute-start.10 = (bf16[2,2,64,3200]{3,2,1,0:T(8,128)(2,1)S(1)}, bf16[2,2,64,3200]{3,2,1,0:T(8,128)(2,1)S(1)}, u32[]{:S(2)}, u32[]{:S(2)}) collective-permute-start(bf16[2,2,64,3200]{3,2,1,0:T(8,128)(2,1)S(1)} %collective-permute-done.6.refs_3_), channel_id=1, source_target_pairs={{0,1},{1,0},{2,3},{3,2},{4,5},{5,4},{6,7},{7,6},{8,9},{9,8},{10,11... | collective-permute-start | bytes 4915208 | tf_op jit(solution)/shard_map/ppermute | solution.py:541
  313.1 57.4 %collective-permute-start.15 = (bf16[2,2,64,3200]{3,2,1,0:T(8,128)(2,1)}, bf16[2,2,64,3200]{3,2,1,0:T(8,128)(2,1)}, u32[]{:S(2)}, u32[]{:S(2)}) collective-permute-start(bf16[2,2,64,3200]{3,2,1,0:T(8,128)(2,1)} %get-tuple-element.110.refs_4_), channel_id=1, source_target_pairs={{0,6},{1,7},{2,4},{3,5},{4,2},{5,3},{6,0},{7,1},{8,14},{9,15},{10,... | collective-permute-start | bytes 4915208 | tf_op jit(solution)/shard_map/ppermute | solution.py:534
  314.6 55.9 %collective-permute-start.14 = (bf16[2,2,64,3200]{3,2,1,0:T(8,128)(2,1)}, bf16[2,2,64,3200]{3,2,1,0:T(8,128)(2,1)}, u32[]{:S(2)}, u32[]{:S(2)}) collective-permute-start(bf16[2,2,64,3200]{3,2,1,0:T(8,128)(2,1)} %get-tuple-element.110.refs_4_), channel_id=1, source_target_pairs={{0,2},{1,3},{2,0},{3,1},{4,6},{5,7},{6,4},{7,5},{8,10},{9,11},{10,... | collective-permute-start | bytes 4915208 | tf_op jit(solution)/shard_map/ppermute | solution.py:534
  315.8 26.6 %collective-permute-start.9 = (bf16[2,1,1600,128]{3,2,1,0:T(8,128)(2,1)S(1)}, bf16[2,1,1600,128]{3,2,1,0:T(8,128)(2,1)S(1)}, u32[]{:S(2)}, u32[]{:S(2)}) collective-permute-start(bf16[2,1,1600,128]{3,2,1,0:T(8,128)(2,1)S(1)} %collective-permute-done.5.refs_2_), channel_id=1, source_target_pairs={{0,1},{1,0},{2,3},{3,2},{4,5},{5,4},{6,7},{7,6},{8,9},{9,8},{10,11... | collective-permute-start | bytes 2457608 | tf_op jit(solution)/shard_map/ppermute | solution.py:541
  342.4 28.1 %collective-permute-start.13 = (bf16[2,1,1600,128]{3,2,1,0:T(8,128)(2,1)S(1)}, bf16[2,1,1600,128]{3,2,1,0:T(8,128)(2,1)S(1)}, u32[]{:S(2)}, u32[]{:S(2)}) collective-permute-start(bf16[2,1,1600,128]{3,2,1,0:T(8,128)(2,1)S(1)} %bitcast.49), channel_id=1, source_target_pairs={{0,6},{1,7},{2,4},{3,5},{4,2},{5,3},{6,0},{7,1},{8,14},{9,15},{10,... | collective-permute-start | bytes 2457608 | tf_op jit(solution)/shard_map/ppermute | solution.py:534
  344.0 26.5 %collective-permute-start.12 = (bf16[2,1,1600,128]{3,2,1,0:T(8,128)(2,1)S(1)}, bf16[2,1,1600,128]{3,2,1,0:T(8,128)(2,1)S(1)}, u32[]{:S(2)}, u32[]{:S(2)}) collective-permute-start(bf16[2,1,1600,128]{3,2,1,0:T(8,128)(2,1)S(1)} %bitcast.50), channel_id=1, source_target_pairs={{0,2},{1,3},{2,0},{3,1},{4,6},{5,7},{6,4},{7,5},{8,10},{9,11},{10,... | collective-permute-start | bytes 2457608 | tf_op jit(solution)/shard_map/ppermute | solution.py:534
  371.4 62.5 %collective-permute-start.20 = (bf16[1,1600,128]{2,1,0:T(8,128)(2,1)}, bf16[1,1600,128]{2,1,0:T(8,128)(2,1)}, u32[]{:S(2)}, u32[]{:S(2)}) collective-permute-start(bf16[1,1600,128]{2,1,0:T(8,128)(2,1)} %slice_bitcast_fusion.7), channel_id=1, source_target_pairs={{0,2},{1,3},{2,0},{3,1},{4,6},{5,7},{6,4},{7,5},{8,10},{9,11},{10,... | collective-permute-start | bytes 1228808 | tf_op jit(solution)/shard_map/ppermute | solution.py:540
  374.3 33.1 %collective-permute-start.19 = (bf16[2,2,64,3200]{3,2,1,0:T(8,128)(2,1)}, bf16[2,2,64,3200]{3,2,1,0:T(8,128)(2,1)S(1)}, u32[]{:S(2)}, u32[]{:S(2)}) collective-permute-start(bf16[2,2,64,3200]{3,2,1,0:T(8,128)(2,1)} %collective-permute-done.15.refs_4_), channel_id=1, source_target_pairs={{0,1},{1,0},{2,3},{3,2},{4,5},{5,4},{6,7},{7,6},{8,9},{9,8},{10,11... | collective-permute-start | bytes 4915208 | tf_op jit(solution)/shard_map/ppermute | solution.py:541
  376.7 58.9 %collective-permute-start.21 = (bf16[1,1600,128]{2,1,0:T(8,128)(2,1)}, bf16[1,1600,128]{2,1,0:T(8,128)(2,1)}, u32[]{:S(2)}, u32[]{:S(2)}) collective-permute-start(bf16[1,1600,128]{2,1,0:T(8,128)(2,1)} %slice_bitcast_fusion.6), channel_id=1, source_target_pairs={{0,6},{1,7},{2,4},{3,5},{4,2},{5,3},{6,0},{7,1},{8,14},{9,15},{10,... | collective-permute-start | bytes 1228808 | tf_op jit(solution)/shard_map/ppermute | solution.py:540
  378.3 57.3 %collective-permute-start.22 = (bf16[2,64,3200]{2,1,0:T(8,128)(2,1)}, bf16[2,64,3200]{2,1,0:T(8,128)(2,1)}, u32[]{:S(2)}, u32[]{:S(2)}) collective-permute-start(bf16[2,64,3200]{2,1,0:T(8,128)(2,1)} %slice_bitcast_fusion.3), channel_id=1, source_target_pairs={{0,2},{1,3},{2,0},{3,1},{4,6},{5,7},{6,4},{7,5},{8,10},{9,11},{10,... | collective-permute-start | bytes 2457608 | tf_op jit(solution)/shard_map/ppermute | solution.py:540
  378.3 57.3 %collective-permute-start.23 = (bf16[2,64,3200]{2,1,0:T(8,128)(2,1)}, bf16[2,64,3200]{2,1,0:T(8,128)(2,1)}, u32[]{:S(2)}, u32[]{:S(2)}) collective-permute-start(bf16[2,64,3200]{2,1,0:T(8,128)(2,1)} %slice_bitcast_fusion.2), channel_id=1, source_target_pairs={{0,6},{1,7},{2,4},{3,5},{4,2},{5,3},{6,0},{7,1},{8,14},{9,15},{10,... | collective-permute-start | bytes 2457608 | tf_op jit(solution)/shard_map/ppermute | solution.py:540
  407.4 64.2 %collective-permute-start.30 = (bf16[2,64,3200]{2,1,0:T(8,128)(2,1)}, bf16[2,64,3200]{2,1,0:T(8,128)(2,1)}, u32[]{:S(2)}, u32[]{:S(2)}) collective-permute-start(bf16[2,64,3200]{2,1,0:T(8,128)(2,1)} %slice_bitcast_fusion.1), channel_id=1, source_target_pairs={{0,2},{1,3},{2,0},{3,1},{4,6},{5,7},{6,4},{7,5},{8,10},{9,11},{10,... | collective-permute-start | bytes 2457608 | tf_op jit(solution)/shard_map/ppermute | solution.py:540
  433.9 37.8 %collective-permute-start.31 = (bf16[2,64,3200]{2,1,0:T(8,128)(2,1)}, bf16[2,64,3200]{2,1,0:T(8,128)(2,1)}, u32[]{:S(2)}, u32[]{:S(2)}) collective-permute-start(bf16[2,64,3200]{2,1,0:T(8,128)(2,1)} %slice_bitcast_fusion), channel_id=1, source_target_pairs={{0,6},{1,7},{2,4},{3,5},{4,2},{5,3},{6,0},{7,1},{8,14},{9,15},{10,... | collective-permute-start | bytes 2457608 | tf_op jit(solution)/shard_map/ppermute | solution.py:540
  437.4 18.8 %collective-permute-start.27 = (bf16[2,64,3200]{2,1,0:T(8,128)(2,1)}, bf16[2,64,3200]{2,1,0:T(8,128)(2,1)S(1)}, u32[]{:S(2)}, u32[]{:S(2)}) collective-permute-start(bf16[2,64,3200]{2,1,0:T(8,128)(2,1)} %collective-permute-done.23.refs_4_), channel_id=1, source_target_pairs={{0,1},{1,0},{2,3},{3,2},{4,5},{5,4},{6,7},{7,6},{8,9},{9,8},{10,11... | collective-permute-start | bytes 2457608 | tf_op jit(solution)/shard_map/ppermute | solution.py:546
  439.2 32.5 %collective-permute-start.28 = (bf16[1,1600,128]{2,1,0:T(8,128)(2,1)}, bf16[1,1600,128]{2,1,0:T(8,128)(2,1)}, u32[]{:S(2)}, u32[]{:S(2)}) collective-permute-start(bf16[1,1600,128]{2,1,0:T(8,128)(2,1)} %slice_bitcast_fusion.5), channel_id=1, source_target_pairs={{0,2},{1,3},{2,0},{3,1},{4,6},{5,7},{6,4},{7,5},{8,10},{9,11},{10,... | collective-permute-start | bytes 1228808 | tf_op jit(solution)/shard_map/ppermute | solution.py:540
  439.3 32.4 %collective-permute-start.29 = (bf16[1,1600,128]{2,1,0:T(8,128)(2,1)}, bf16[1,1600,128]{2,1,0:T(8,128)(2,1)}, u32[]{:S(2)}, u32[]{:S(2)}) collective-permute-start(bf16[1,1600,128]{2,1,0:T(8,128)(2,1)} %slice_bitcast_fusion.4), channel_id=1, source_target_pairs={{0,6},{1,7},{2,4},{3,5},{4,2},{5,3},{6,0},{7,1},{8,14},{9,15},{10,... | collective-permute-start | bytes 1228808 | tf_op jit(solution)/shard_map/ppermute | solution.py:540
  471.7 16.5 %collective-permute-start.34 = (bf16[2,64,3200]{2,1,0:T(8,128)(2,1)}, bf16[2,64,3200]{2,1,0:T(8,128)(2,1)S(1)}, u32[]{:S(2)}, u32[]{:S(2)}) collective-permute-start(bf16[2,64,3200]{2,1,0:T(8,128)(2,1)} %collective-permute-done.30.refs_3_), channel_id=1, source_target_pairs={{0,1},{1,0},{2,3},{3,2},{4,5},{5,4},{6,7},{7,6},{8,9},{9,8},{10,11... | collective-permute-start | bytes 2457608 | tf_op jit(solution)/shard_map/ppermute | solution.py:546
  471.8 16.4 %collective-permute-start.35 = (bf16[2,64,3200]{2,1,0:T(8,128)(2,1)}, bf16[2,64,3200]{2,1,0:T(8,128)(2,1)S(1)}, u32[]{:S(2)}, u32[]{:S(2)}) collective-permute-start(bf16[2,64,3200]{2,1,0:T(8,128)(2,1)} %collective-permute-done.31.refs_4_), channel_id=1, source_target_pairs={{0,1},{1,0},{2,3},{3,2},{4,5},{5,4},{6,7},{7,6},{8,9},{9,8},{10,11... | collective-permute-start | bytes 2457608 | tf_op jit(solution)/shard_map/ppermute | solution.py:546
  472.3 15.9 %collective-permute-start.32 = (bf16[1,1600,128]{2,1,0:T(8,128)(2,1)}, bf16[1,1600,128]{2,1,0:T(8,128)(2,1)S(1)}, u32[]{:S(2)}, u32[]{:S(2)}) collective-permute-start(bf16[1,1600,128]{2,1,0:T(8,128)(2,1)} %collective-permute-done.28.refs_1_), channel_id=1, source_target_pairs={{0,1},{1,0},{2,3},{3,2},{4,5},{5,4},{6,7},{7,6},{8,9},{9,8},{10,11... | collective-permute-start | bytes 1228808 | tf_op jit(solution)/shard_map/ppermute | solution.py:546
  (17 other events, 138.1 us)

commit v2 on v1

--- a/solution.py
+++ b/solution.py
@@ -7,29 +7,12 @@
 from jax.experimental.pallas import tpu as pltpu
 from jax.sharding import PartitionSpec as P
 
-NAMES = ("w_gate", "w_up", "w_down")
+
 SLOTS = 4
 
 
-def matmul(a, w):
-    return jnp.dot(a, w, preferred_element_type=jnp.float32).astype(jnp.bfloat16)
-
-
-def normed(h):
-    wide = h.astype(jnp.float32)
-    scale = lax.rsqrt(jnp.mean(wide**2, -1, keepdims=True) + 1e-6)
-    return (wide * scale).astype(jnp.bfloat16)
-
-
-def layer(h, w):
-    a = normed(h)
-    gate = jnp.dot(a, w["w_gate"], preferred_element_type=jnp.float32)
-    up = jnp.dot(a, w["w_up"], preferred_element_type=jnp.float32)
-    return h + matmul((jax.nn.silu(gate) * up).astype(jnp.bfloat16), w["w_down"])
-
-
 MESH = pl.DeviceIdType.MESH
-DEEP = 3
+DEEP = 4
 TILES = 5
 
 
@@ -41,28 +24,23 @@
 
 
 def backward_kernel(
-    n, layers, x_ref, *refs
+    n, layers, x_ref, dy_ref, wg_ref, wu_ref, wd_ref, *refs
 ):
-    inner, refs = refs[: layers - 1], refs[layers - 1 :]
-    dy_ref, wg_ref, wu_ref, wd_ref, refs = *refs[:4], refs[4:]
-    gu_outs, d_outs, factor_ref, refs = refs[:layers], refs[layers : 2 * layers], refs[2 * layers], refs[2 * layers + 1 :]
-    (h, a, aT, dh, dhT, wg, wu, wd, act, dgate, dup, acc_g, acc_u, send0, own, rcv0, rcv1, rcv2, fin, squares, parts,
+    outs, factor_ref, refs = refs[: 2 * layers], refs[2 * layers], refs[2 * layers + 1 :]
+    (hs, a, aT, dh, wg, wu, wd, actT, dgate, dup, acc_g, acc_u, send0, own, rcv0, rcv1, rcv2, fin, squares, parts,
      w_sem, h_sem, send0_sem, rcv0_sem, send1_sem, rcv1_sem, send2_sem, rcv2_sem, fin_sem, ssend_sem, srecv_sem,
      credit_p, credit_a, credit_b) = refs
     me, c, x, xa, xb, xo = hops()
     peer, to_a, to_b = 2 * x + 1 - c, 2 * xa + c, 2 * xb + c
-    tokens, depth = h.shape
+    tokens, depth = dh.shape
     width = wg.shape[-1]
     steps = layers * TILES
     half = depth // 2
-    tall = 256
-    inputs = (x_ref, *inner)
-
-    def load_h(number):
-        return pltpu.make_async_copy(inputs[number], h, h_sem.at[0])
-
-    def weights_of(s):
-        number, j, slot = layers - 1 - s // TILES, s % TILES, s % 2
+    ahead = (layers - 1) * TILES
+    tall = 512
+
+    def weights_of(t, number):
+        j, slot = t % TILES, t % 2
         at = pl.ds(pl.multiple_of(j * width, width), width)
         return [
             pltpu.make_async_copy(wg_ref.at[number, :, at], wg.at[slot], w_sem.at[0, slot]),
@@ -76,7 +54,7 @@
             at = pl.ds(pl.multiple_of(r * 128, 128), 128)
             target[:, at] = source[at, :].T
 
-    def norm():
+    def norm(h):
         @pl.loop(0, tokens // 64)
         def _(r):
             at = pl.ds(pl.multiple_of(r * 64, 64), 64)
@@ -84,10 +62,11 @@
             scale = lax.rsqrt(jnp.mean(wide**2, -1, keepdims=True) + 1e-6)
             a[at] = (wide * scale).astype(jnp.bfloat16)
 
-    load_h(layers - 1).start()
+    first_h = pltpu.make_async_copy(x_ref, hs.at[0], h_sem.at[0])
+    first_h.start()
     first_dh = pltpu.make_async_copy(dy_ref, dh, h_sem.at[1])
     first_dh.start()
-    for one in weights_of(0):
+    for one in weights_of(0, 0):
         one.start()
 
     barrier = pltpu.get_barrier_semaphore()
@@ -95,11 +74,36 @@
         pl.semaphore_signal(barrier, inc=1, device_id={"dp": (me + k) % n}, device_id_type=MESH)
     pl.semaphore_wait(barrier, n - 1)
 
-    load_h(layers - 1).wait()
-    norm()
+    first_h.wait()
+
+    for number in range(layers - 1):
+        norm(hs.at[number])
+        acc_g[...] = jnp.zeros_like(acc_g)
+
+        @pl.loop(number * TILES, (number + 1) * TILES)
+        def _(t):
+            slot = t % 2
+            for one in weights_of(t, number):
+                one.wait()
+            for one in weights_of(t + 1, (t + 1) // TILES):
+                one.start()
+
+            @pl.loop(0, tokens // tall)
+            def _(r):
+                at = pl.ds(pl.multiple_of(r * tall, tall), tall)
+                gate = jnp.dot(a[at], wg[slot], preferred_element_type=jnp.float32)
+                up = jnp.dot(a[at], wu[slot], preferred_element_type=jnp.float32)
+                dup[at] = (gate * jax.nn.sigmoid(gate) * up).astype(jnp.bfloat16)
+                acc_g[at] += jnp.dot(dup[at], wd[slot], preferred_element_type=jnp.float32)
+
+        @pl.loop(0, tokens // 64)
+        def _(r):
+            at = pl.ds(pl.multiple_of(r * 64, 64), 64)
+            hs[number + 1, at] = hs[number, at] + acc_g[at].astype(jnp.bfloat16)
+
+    norm(hs.at[layers - 1])
     turn(a, aT)
     first_dh.wait()
-    turn(dh, dhT)
 
     def remote(source, target, sends, receives, to):
         return pltpu.make_async_remote_copy(
@@ -158,10 +162,7 @@
 
     def fin_copies(s, number):
         at = pl.ds(pl.multiple_of((s % TILES) * width, width), width)
-        return [
-            pltpu.make_async_copy(fin.at[:, 0:2], gu_outs[number].at[:, :, :, at], fin_sem.at[0]),
-            pltpu.make_async_copy(fin.at[:, 2], d_outs[number].at[:, :, at], fin_sem.at[1]),
-        ]
+        return [pltpu.make_async_copy(fin.at[colour], outs[2 * number + colour].at[:, :, at], fin_sem.at[colour]) for colour in range(2)]
 
     def finish(s):
         for *_, one in step_two(s):
@@ -202,22 +203,33 @@
         def _(r):
             at = pl.ds(pl.multiple_of(core * half + r * tall, tall), tall)
             blocks = tall // 64
-            for mat, (left, right) in enumerate(((aT, dgate), (aT, dup), (dhT, act))):
-                got = jnp.dot(left[at], right[...], preferred_element_type=jnp.float32).astype(jnp.bfloat16)
+            for mat, right in enumerate((dgate, dup)):
+                got = jnp.dot(aT[at], right[...], preferred_element_type=jnp.float32).astype(jnp.bfloat16)
                 for b in range(blocks):
-                    keep(r * blocks + b, mat, got[b * 64 : (b + 1) * 64])
+                    keep((r * blocks + b, mat), got[b * 64 : (b + 1) * 64])
+            rows = width // 2 // for_rows
+            at = pl.ds(pl.multiple_of(core * (width // 2) + r * rows, rows), rows)
+            got = jnp.dot(actT[at], dh[...], preferred_element_type=jnp.float32).astype(jnp.bfloat16)
+            rows = width // 8
+            for b in range(blocks):
+                for i in range(rows // 16):
+                    for k in range(4):
+                        row, col = b // 2 * rows + i * 16, b % 2 * (depth // 2) + k * 128
+                        place = (r * blocks + b, 2, pl.ds(k * 16, 16), pl.ds(i * 128, 128))
+                        keep(place, got[row : row + 16, col : col + 128])
 
     squares[...] = jnp.zeros_like(squares)
 
     @pl.loop(0, steps)
     def _(s):
-        slot, k = s % 2, s % DEEP
-        for one in weights_of(s):
+        t, even, k = s + ahead, s % 2, s % DEEP
+        slot = t % 2
+        for one in weights_of(t, layers - 1 - s // TILES):
             one.wait()
 
         @pl.when(s + 1 < steps)
         def _():
-            for one in weights_of(s + 1):
+            for one in weights_of(t + 1, layers - 1 - (s + 1) // TILES):
                 one.start()
 
         @pl.loop(0, tokens // tall)
@@ -229,7 +241,7 @@
             by_act = by_act.astype(jnp.bfloat16).astype(jnp.float32)
             share = jax.nn.sigmoid(gate)
             silu = gate * share
-            act[at] = (silu * up).astype(jnp.bfloat16)
+            actT[:, at] = (silu * up).astype(jnp.bfloat16).T
             dup[at] = (by_act * silu).astype(jnp.bfloat16)
             dgate[at] = (by_act * up * (share + silu * (1.0 - share))).astype(jnp.bfloat16)
 
@@ -237,8 +249,8 @@
         def _():
             swap(s).wait_send()
 
-        def to_send(b, mat, value):
-            send0[slot, b, mat] = value
+        def to_send(place, value):
+            send0[even, *place] = value
 
         gradients(1 - c, to_send)
 
@@ -248,8 +260,8 @@
 
         swap(s).start()
 
-        def to_own(b, mat, value):
-            own[k, b, mat] = value
+        def to_own(place, value):
+            own[k, *place] = value
 
         gradients(c, to_own)
         begin(s)
@@ -258,9 +270,9 @@
         def _():
             pass_on(s - 1)
 
-        @pl.when(s >= 2)
-        def _():
-            finish(s - 2)
+        @pl.when(s >= DEEP - 1)
+        def _():
+            finish(s - (DEEP - 1))
 
         @pl.when(s < steps - TILES)
         def _():
@@ -281,26 +293,18 @@
                 def _(r):
                     at = pl.ds(pl.multiple_of(r * 32, 32), 32)
                     by = acc_g[at].astype(jnp.bfloat16) + acc_u[at].astype(jnp.bfloat16)
-                    by, wide = by.astype(jnp.float32), h[at].astype(jnp.float32)
+                    by, wide = by.astype(jnp.float32), hs[layers - 1 - s // TILES, at].astype(jnp.float32)
                     scale = lax.rsqrt(jnp.mean(wide**2, -1, keepdims=True) + 1e-6)
                     inner = jnp.mean(by * wide, -1, keepdims=True)
                     by_h = (by * scale - wide * (scale * scale * scale * inner)).astype(jnp.bfloat16)
                     dh[at] = dh[at] + by_h
 
-                for number in range(layers - 1):
-
-                    @pl.when(layers - 2 - s // TILES == number)
-                    def _():
-                        load_h(number).start()
-                        load_h(number).wait()
-
-                norm()
+                norm(hs.at[layers - 2 - s // TILES])
                 turn(a, aT)
-                turn(dh, dhT)
 
     pass_on(jnp.int32(steps - 1))
-    finish(jnp.int32(steps - 2))
-    finish(jnp.int32(steps - 1))
+    for back in range(DEEP - 1, 0, -1):
+        finish(jnp.int32(steps - back))
     for one in fin_copies(jnp.int32(steps - 1), 0):
         one.wait()
     swap(jnp.int32(steps - 2)).wait_send()
@@ -322,28 +326,26 @@
     factor_ref[...] = jnp.minimum(1.0, 0.5 * lax.rsqrt(jnp.full(factor_ref.shape, jnp.sum(total)) / count + 1e-30))
 
 
-def backward(n, inputs, dy, weights):
+def backward(n, x, dy, weights):
     layers, depth, hidden = weights[0].shape
     tokens, width, rows = dy.shape[0], hidden // TILES, depth // 16
     bf16, dma, regular = jnp.bfloat16, pltpu.SemaphoreType.DMA, pltpu.SemaphoreType.REGULAR
     any_spec = pl.BlockSpec(memory_space=pl.ANY)
     out = pl.pallas_call(
         functools.partial(backward_kernel, n, layers),
-        out_shape=[jax.ShapeDtypeStruct((2, 2, rows, hidden), bf16)] * layers
-        + [jax.ShapeDtypeStruct((2, rows, hidden), bf16)] * layers
+        out_shape=[jax.ShapeDtypeStruct((3, rows, hidden), bf16)] * (2 * layers)
         + [jax.ShapeDtypeStruct((8, 128), jnp.float32)],
-        in_specs=[any_spec] * (layers + 4),
+        in_specs=[any_spec] * 5,
         out_specs=[any_spec] * (2 * layers) + [pl.BlockSpec(memory_space=pltpu.VMEM)],
         scratch_shapes=[
-            pltpu.VMEM((tokens, depth), bf16),
+            pltpu.VMEM((layers, tokens, depth), bf16),
             pltpu.VMEM((tokens, depth), bf16),
             pltpu.VMEM((depth, tokens), bf16),
             pltpu.VMEM((tokens, depth), bf16),
-            pltpu.VMEM((depth, tokens), bf16),
             pltpu.VMEM((2, depth, width), bf16),
             pltpu.VMEM((2, depth, width), bf16),
             pltpu.VMEM((2, width, depth), bf16),
-            pltpu.VMEM((tokens, width), bf16),
+            pltpu.VMEM((width, tokens), bf16),
             pltpu.VMEM((tokens, width), bf16),
             pltpu.VMEM((tokens, width), bf16),
             pltpu.VMEM((tokens, depth), jnp.float32),
@@ -373,8 +375,8 @@
         ],
         compiler_params=pltpu.CompilerParams(collective_id=0, has_side_effects=True, vmem_limit_bytes=67_043_328),
         cost_estimate=pl.CostEstimate(flops=16 * tokens * depth * hidden * layers, bytes_accessed=2**27, transcendentals=0),
-    )(*inputs, dy, *weights)
-    return out[:layers], out[layers : 2 * layers], out[-1]
+    )(x, dy, *weights)
+    return out[:-1], out[-1]
 
 
 def update_kernel(items, n_new, *refs):
@@ -389,18 +391,17 @@
     c, x = place()
     copy = pltpu.make_async_copy(factor_ref, factor_vmem, f_sem)
     copy.start()
-    copy.wait()
-    factor = factor_vmem[0:1, 0:1]
 
     def views(n):
         which, tile, weight, layer, core, rel, colour = items[n]
         slot = n % SLOTS
         buffers = [b.at[slot] for b in (tall if weight == 2 else wide)]
-        rows, cols = buffers[0].shape
         owner = spot(c, x, core, rel)
         if weight == 2:
-            index = (layer, pl.ds(colour * rows, rows), pl.ds(pl.multiple_of(owner * cols, cols), cols))
+            rows, cols = buffers[0].shape[1:]
+            index = (layer, slice(None), pl.ds(pl.multiple_of(owner * rows, rows), rows), pl.ds(colour * cols, cols))
         else:
+            rows = buffers[0].shape[0]
             index = (layer, pl.ds(pl.multiple_of((owner * 2 + colour) * rows, rows), rows))
         sources = [old[3 * j + weight].at[index] for j in range(3)] + [g_refs[which].at[tile]]
         targets = [new[3 * j + weight].at[index] for j in range(3)]
@@ -418,6 +419,8 @@
     for n in range(min(ahead, len(items))):
         for one in loads(n):
             one.start()
+    copy.wait()
+    factor = factor_vmem[0:1, 0:1]
     for n in range(len(items)):
         if n + ahead < len(items):
             if n + ahead - SLOTS >= 0:
@@ -428,22 +431,35 @@
         for one in loads(n):
             one.wait()
         w_ref, m_ref, v_ref, g_ref = views(n)[0]
-        rows, cols = w_ref.shape
-        across = cols // 5 if cols % 5 == 0 else cols
-
-        @pl.loop(0, rows // 16)
-        def _(r):
-            at = pl.ds(pl.multiple_of(r * 16, 16), 16)
-            for k in range(cols // across):
-                lanes = pl.ds(k * across, across)
-                g = g_ref[at, lanes].astype(jnp.float32) * factor
-                m = 0.9 * m_ref[at, lanes] + 0.1 * g
-                v = 0.95 * v_ref[at, lanes] + 0.05 * g * g
-                w = w_ref[at, lanes].astype(jnp.float32)
-                move = m * lax.rsqrt(v + 1e-8) + 0.1 * w
-                w_ref[at, lanes] = (w - 0.02 * move).astype(jnp.bfloat16)
-                m_ref[at, lanes] = m
-                v_ref[at, lanes] = v
+
+        def move(place, g):
+            g = g.astype(jnp.float32) * factor
+            m = 0.9 * m_ref[place] + 0.1 * g
+            v = 0.95 * v_ref[place] + 0.05 * g * g
+            w = w_ref[place].astype(jnp.float32)
+            step = m * lax.rsqrt(v + 1e-8) + 0.1 * w
+            w_ref[place] = (w - 0.02 * step).astype(jnp.bfloat16)
+            m_ref[place] = m
+            v_ref[place] = v
+
+        if items[n][2] == 2:
+            tiles, rows = w_ref.shape[:2]
+
+            @pl.loop(0, tiles * (rows // 16))
+            def _(r):
+                for k in range(g_ref.shape[0] // 16):
+                    place = (r // (rows // 16), pl.ds(pl.multiple_of(r % (rows // 16) * 16, 16), 16), pl.ds(k * 128, 128))
+                    move(place, g_ref[pl.ds(k * 16, 16), pl.ds(pl.multiple_of(r * 128, 128), 128)])
+        else:
+            rows, cols = w_ref.shape
+            across = cols // TILES
+
+            @pl.loop(0, rows // 16)
+            def _(r):
+                at = pl.ds(pl.multiple_of(r * 16, 16), 16)
+                for k in range(TILES):
+                    place = (at, pl.ds(k * across, across))
+                    move(place, g_ref[place])
 
         for one in stores(n):
             one.start()
@@ -464,11 +480,12 @@
 
 def update(factor, items, gs, old, new):
     rows, cols = old[0].shape[1:]
-    down_rows, down_cols = old[2].shape[1:]
-    wide, tall = (rows // 16, cols), (down_rows // 2, down_cols // 8)
+    tiles, down_rows, down_cols = old[2].shape[1:]
+    wide, tall = (rows // 16, cols), (tiles, down_rows // 8, down_cols // 2)
+    bf16, wider = jnp.bfloat16, jnp.float32
 
     def slots(shape):
-        return [pltpu.VMEM((SLOTS, *shape), t) for t in (jnp.bfloat16, jnp.float32, jnp.float32, jnp.bfloat16)]
+        return [pltpu.VMEM((SLOTS, *one), t) for one, t in ((shape, bf16), (shape, wider), (shape, wider), (wide, bf16))]
 
     any_spec = pl.BlockSpec(memory_space=pl.ANY)
     n_in = 1 + len(gs) + 9 + (9 if new is not None else 0)
@@ -488,7 +505,7 @@
         ],
         input_output_aliases={} if new is None else {n_in - 9 + i: i for i in range(9)},
         cost_estimate=pl.CostEstimate(flops=size * 400, bytes_accessed=size * 22, transcendentals=size),
-        compiler_params=pltpu.CompilerParams(vmem_limit_bytes=32 * 2**20),
+        compiler_params=pltpu.CompilerParams(vmem_limit_bytes=62 * 2**20),
     )(factor, *gs, *old, *(new if new is not None else ()))
 
 
@@ -500,52 +517,53 @@
     peers = [(i, i ^ 1) for i in range(n)]
     to_a, to_b, to_peer = (functools.partial(lax.ppermute, axis_name="dp", perm=perm) for perm in (pair_a, pair_b, peers))
 
+    def gather(shards, factor, arrays):
+        layers = arrays[0].shape[0]
+        calls = []
+
+        arrays = [w.reshape(layers, TILES, w.shape[1] // TILES, w.shape[2]) if i % 3 == 2 else w for i, w in enumerate(arrays)]
+
+        def run(new, parts):
+            items = []
+            for i, (unit, _, core, rel) in enumerate(parts):
+                number, colour, _ = shards[unit]
+                items += [(i, mat, mat, number, core, rel, colour) for mat in range(3)]
+            calls.append(len(calls))
+            return update(factor, items, [g for _, g, _, _ in parts], arrays, new)
+
+        def after(new, waited):
+            first, waited = lax.optimization_barrier((new[0], waited))
+            return [first, *new[1:]], waited
+
+        near = []
+        for _, _, own in shards:
+            one = to_a(own)
+            near.append((one, to_b(own)))
+        beside = [to_peer(own) for _, _, own in shards]
+        new = run(None, [(u, own, 0, 0) for u, (_, _, own) in enumerate(shards)] + [(u, g, 1, 0) for u, g in enumerate(beside)])
+        far, waiting = [], []
+        for u, (_, colour, _) in enumerate(shards):
+            new, got = after(new, near[u])
+            far.append(to_b(got[0]) if colour else to_a(got[1]))
+            across = [(u, to_peer(g), 1, 1 + j) for j, g in enumerate(got)]
+            new = run(new, [(u, g, 0, 1 + j) for j, g in enumerate(got)] + waiting)
+            waiting = across
+        for u, g in enumerate(far):
+            new, got = after(new, g)
+            across = [(u, to_peer(got), 1, 3)]
+            new = run(new, waiting + [(u, got, 0, 3)])
+            waiting = across
+        new = run(new, waiting)
+        return new
+
     def step(x, dy, *arrays):
         weights = arrays[:3]
         layers = weights[0].shape[0]
-        h, kept = x[0], []
-        for number in range(layers):
-            kept.append(h)
-            if number < layers - 1:
-                h = layer(h, {name: w[number] for name, w in zip(NAMES, weights, strict=True)})
-        wide, tall, factor = backward(n, kept, dy[0], weights)
-        shards = []
-        for number in reversed(range(layers)):
-            down = tall[number].reshape(-1, tall[number].shape[-1]).T
-            shards.append((number, 2, down.reshape(2, 1, down.shape[0] // 2, down.shape[1])))
-            shards.append((number, 0, wide[number]))
-
-        def run(new, parts):
-            items, gs = [], []
-            for unit, g, core, rel, colour in parts:
-                number, weight, own = shards[unit]
-                for this in range(2) if colour is None else (colour,):
-                    for kind in range(own.shape[1]):
-                        tile = (this, kind) if colour is None else (kind,)
-                        items.append((len(gs), tile, weight + kind, number, core, rel, this))
-                gs.append(g)
-            return update(factor, items, gs, arrays, new)
-
-        def after(new, waited):
-            first, waited = lax.optimization_barrier((new[0], waited))
-            return [first, *new[1:]], waited
-
-        owns = [own for _, _, own in shards]
-        near = [(to_a(own), to_b(own)) for own in owns]
-        beside = [to_peer(own) for own in owns]
-        new = run(None, [(u, own, 0, 0, None) for u, own in enumerate(owns)] + [(u, g, 1, 0, None) for u, g in enumerate(beside)])
-        groups, far = [(0, 1), (2, 3)], []
-        for i, group in enumerate(groups):
-            new, got = after(new, [near[u] for u in group])
-            far.append([(to_a(from_b[0]), to_b(from_a[1])) for from_a, from_b in got])
-            beside = [(to_peer(from_a), to_peer(from_b)) for from_a, from_b in got]
-            new = run(new, [(u, g, 0, 1 + j, None) for u, pair in zip(group, got, strict=True) for j, g in enumerate(pair)])
-            new = run(new, [(u, g, 1, 1 + j, None) for u, pair in zip(group, beside, strict=True) for j, g in enumerate(pair)])
-        for i, group in enumerate(groups):
-            new, got = after(new, far[i])
-            beside = [(to_peer(over_a), to_peer(over_b)) for over_a, over_b in got]
-            new = run(new, [(u, g, 0, 3, j) for u, pair in zip(group, got, strict=True) for j, g in enumerate(pair)])
-            new = run(new, [(u, g, 1, 3, j) for u, pair in zip(group, beside, strict=True) for j, g in enumerate(pair)])
+        blocks, factor = backward(n, x[0], dy[0], weights)
+        shards = [(number, colour, blocks[2 * number + colour]) for number in reversed(range(layers)) for colour in range(2)]
+
+        new = gather(shards, factor, arrays)
+        new = [o.reshape(o.shape[0], -1, o.shape[-1]) for o in new]
         return tuple(new)
 
     return jax.shard_map(

time: 505 us -> 450 us (0.89)
  matrix products: 36.1 us -> 0 us
  waiting for transfers between devices: 2.91 us -> 29.2 us
  Pallas kernels: 419 us -> 398 us
  local copies, waits for them, and re-layouts: 19.5 us -> 3.18 us
  starting transfers between devices: 23.4 us -> 17.6 us
    pallas_call x9 -> x10, Pallas kernels: 207 us -> 169 us  [update(): pl.pallas_call(functools.partial(update_kernel, items, new is None), out_...]
    dot_general x2 -> x0, matrix products: 36.1 us -> none  [the longest x1 22.3 us: matmul(): jnp.dot(a, w, preferred_element_type=jnp.float32).astype(jnp.bfloat16)]
    ppermute x36 -> x28, waiting for transfers between devices: 2.91 us -> 29.2 us  [the longest x4 21.1 us: gather(): one = to_a(own)]
    pallas_call x1, Pallas kernels: 211 us -> 229 us  [backward(): pl.pallas_call(functools.partial(backward_kernel, n, layers), out_shape=[...]
    squeeze x8 -> x0, local copies, waits for them, and re-layouts: 9.29 us -> none  [step(): far.append([(to_a(from_b[0]), to_b(from_a[1])) for from_a, from_b in got])]
    ppermute x36 -> x28, starting transfers between devices: 23.4 us -> 17.6 us  [the longest x4 6.18 us: gather(): near.append((one, to_b(own)))]
  transfers between devices with their start and end apart: 36 -> 28, of which waited for: 3 -> 7; matrix products, arithmetic and copies ran while one was open for 3% -> 0% of each run, Pallas kernels for 38% -> 36%
where the time goes in v2:
time: 450 us; the launch traced here: 449 us
  Pallas kernels  398 us (88%)
  waiting for transfers between devices  29.2 us (6%)
  starting transfers between devices  17.6 us (4%)
    pallas_call x1, Pallas kernels, backward(): pl.pallas_call(functools.partial(backward_kernel, n, layers), out_shape=[...  229 us
    pallas_call x10, Pallas kernels, update(): pl.pallas_call(functools.partial(update_kernel, items, new is None), out_...  169 us
    ppermute x4, waiting for transfers between devices, gather(): one = to_a(own)  21.1 us
  transfers between devices with their start and end apart: 28, of which 7 were waited for; matrix products, arithmetic and copies ran while one was open for 0% of the time, Pallas kernels for 36%

profile of v2, /device:TPU:112, one launch (start us, length us, event | category | flops | bytes accessed | tf_op | source)
XLA Modules:
  0.0 449.3 jit_solution(15304863650734052507)
XLA Ops:
  0.6 229.2 %shard_map.178 = (bf16[3,64,3200]{2,1,0:T(8,128)(2,1)}, bf16[3,64,3200]{2,1,0:T(8,128)(2,1)}, bf16[3,64,3200]{2,1,0:T(8,128)(2,1)}, bf16[3,64,3200]{2,1,0:T(8,128)(2,1)}, f32[8,128]{1,0:T(8,128)}) custom-call(bf16[1024,1024]{1,0:T(8,128)(2,1)} %bitcast.41, bf16[1024,1024]{1,0:T(8,128)(2,1)} %bitcast.42, bf16[2,1024,3200]{2,1,0:T(8,128)(2,1)} %refs_2_.1, ...), custom_call_target="tpu_custom_call" | custom-call | flops 107374182400 | bytes 134217728 | tf_op jit(solution)/shard_map/pallas_call | solution.py:334
  231.8 1.4 collective-permute-done.refs_5_
  233.2 1.5 collective-permute-start.5
  236.7 1.5 collective-permute-start.7
  239.3 39.0 %shard_map.179 = (bf16[2,1024,3200]{2,1,0:T(8,128)(2,1)}, bf16[2,1024,3200]{2,1,0:T(8,128)(2,1)}, bf16[2,5,640,1024]{3,2,1,0:T(8,128)(2,1)}, f32[2,1024,3200]{2,...) custom-call(f32[8,128]{1,0:T(8,128)} %get-tuple-element.124.refs_0_,, ...), custom_call_target="tpu_custom_call" | custom-call | flops 1966080000 | bytes 108134400 | tf_op jit(solution)/shard_map/pallas_call | solution.py:493
  279.0 8.6 %collective-permute-done.6.refs_1_ = bf16[3,64,3200]{2,1,0:T(8,128)(2,1)} collective-permute-done((bf16[3,64,3200]{2,1,0:T(8,128)(2,1)}, bf16[3,64,3200]{2,1,0:T(8,128)(2,1)}, u32[]{:S(2)}, u32[]{:S(2)}) %collective-permute-start.6) | collective-permute-done | bytes 1228832 | tf_op jit(solution)/shard_map/ppermute | solution.py:540
  287.5 1.5 collective-permute-start.11
  289.0 11.3 %shard_map.180 = (bf16[2,1024,3200]{2,1,0:T(8,128)(2,1)}, bf16[2,1024,3200]{2,1,0:T(8,128)(2,1)}, bf16[2,5,640,1024]{3,2,1,0:T(8,128)(2,1)}, f32[2,1024,3200]{2,...) custom-call(f32[8,128]{1,0:T(8,128)} %get-tuple-element.124.refs_0_,, ...), custom_call_target="tpu_custom_call", output_to_operand_aliasing={{0}: (12, {}), {1}: (13, {}), {2}: (14, {}), {3}: (15, {}),... | custom-call | flops 491520000 | bytes 27033600 | tf_op jit(solution)/shard_map/pallas_call | solution.py:493
  300.5 12.5 %collective-permute-done.10.refs_1_ = bf16[3,64,3200]{2,1,0:T(8,128)(2,1)} collective-permute-done((bf16[3,64,3200]{2,1,0:T(8,128)(2,1)}, bf16[3,64,3200]{2,1,0:T(8,128)(2,1)}, u32[]{:S(2)}, u32[]{:S(2)}) %collective-permute-start.10) | collective-permute-done | bytes 1228832 | tf_op jit(solution)/shard_map/ppermute | solution.py:540
  313.9 1.6 collective-permute-start.15
  315.5 20.6 %shard_map.181 = (bf16[2,1024,3200]{2,1,0:T(8,128)(2,1)}, bf16[2,1024,3200]{2,1,0:T(8,128)(2,1)}, bf16[2,5,640,1024]{3,2,1,0:T(8,128)(2,1)}, f32[2,1024,3200]{2,...) custom-call(f32[8,128]{1,0:T(8,128)} %get-tuple-element.124.refs_0_,, ...), custom_call_target="tpu_custom_call", output_to_operand_aliasing={{0}: (14, {}), {1}: (15, {}), {2}: (16, {}), {3}: (17, {}),... | custom-call | flops 983040000 | bytes 54067200 | tf_op jit(solution)/shard_map/pallas_call | solution.py:493
  337.2 20.7 %shard_map.182 = (bf16[2,1024,3200]{2,1,0:T(8,128)(2,1)}, bf16[2,1024,3200]{2,1,0:T(8,128)(2,1)}, bf16[2,5,640,1024]{3,2,1,0:T(8,128)(2,1)}, f32[2,1024,3200]{2,...) custom-call(f32[8,128]{1,0:T(8,128)} %get-tuple-element.124.refs_0_,, ...), custom_call_target="tpu_custom_call", output_to_operand_aliasing={{0}: (14, {}), {1}: (15, {}), {2}: (16, {}), {3}: (17, {}),... | custom-call | flops 983040000 | bytes 54067200 | tf_op jit(solution)/shard_map/pallas_call | solution.py:493
  358.5 1.6 collective-permute-start.21
  361.0 20.8 %shard_map.183 = (bf16[2,1024,3200]{2,1,0:T(8,128)(2,1)}, bf16[2,1024,3200]{2,1,0:T(8,128)(2,1)}, bf16[2,5,640,1024]{3,2,1,0:T(8,128)(2,1)}, f32[2,1024,3200]{2,...) custom-call(f32[8,128]{1,0:T(8,128)} %get-tuple-element.124.refs_0_,, ...), custom_call_target="tpu_custom_call", output_to_operand_aliasing={{0}: (14, {}), {1}: (15, {}), {2}: (16, {}), {3}: (17, {}),... | custom-call | flops 983040000 | bytes 54067200 | tf_op jit(solution)/shard_map/pallas_call | solution.py:493
  381.9 1.1 copy-done.1
  383.0 15.8 %shard_map.184 = (bf16[2,1024,3200]{2,1,0:T(8,128)(2,1)}, bf16[2,1024,3200]{2,1,0:T(8,128)(2,1)}, bf16[2,5,640,1024]{3,2,1,0:T(8,128)(2,1)}, f32[2,1024,3200]{2,...) custom-call(f32[8,128]{1,0:T(8,128)} %get-tuple-element.124.refs_0_,, ...), custom_call_target="tpu_custom_call", output_to_operand_aliasing={{0}: (13, {}), {1}: (14, {}), {2}: (15, {}), {3}: (16, {}),... | custom-call | flops 737280000 | bytes 40550400 | tf_op jit(solution)/shard_map/pallas_call | solution.py:493
  399.5 1.3 collective-permute-start.25
  400.8 11.3 %shard_map.185 = (bf16[2,1024,3200]{2,1,0:T(8,128)(2,1)}, bf16[2,1024,3200]{2,1,0:T(8,128)(2,1)}, bf16[2,5,640,1024]{3,2,1,0:T(8,128)(2,1)}, f32[2,1024,3200]{2,...) custom-call(f32[8,128]{1,0:T(8,128)} %get-tuple-element.124.refs_0_,, ...), custom_call_target="tpu_custom_call", output_to_operand_aliasing={{0}: (12, {}), {1}: (13, {}), {2}: (14, {}), {3}: (15, {}),... | custom-call | flops 491520000 | bytes 27033600 | tf_op jit(solution)/shard_map/pallas_call | solution.py:493
  412.3 1.1 copy-done.2
  413.3 11.3 %shard_map.186 = (bf16[2,1024,3200]{2,1,0:T(8,128)(2,1)}, bf16[2,1024,3200]{2,1,0:T(8,128)(2,1)}, bf16[2,5,640,1024]{3,2,1,0:T(8,128)(2,1)}, f32[2,1024,3200]{2,...) custom-call(f32[8,128]{1,0:T(8,128)} %get-tuple-element.124.refs_0_,, ...), custom_call_target="tpu_custom_call", output_to_operand_aliasing={{0}: (12, {}), {1}: (13, {}), {2}: (14, {}), {3}: (15, {}),... | custom-call | flops 491520000 | bytes 27033600 | tf_op jit(solution)/shard_map/pallas_call | solution.py:493
  424.7 5.4 %collective-permute-done.25.refs_2_ = bf16[3,64,3200]{2,1,0:T(8,128)(2,1)} collective-permute-done((bf16[3,64,3200]{2,1,0:T(8,128)(2,1)}, bf16[3,64,3200]{2,1,0:T(8,128)(2,1)}, u32[]{:S(2)}, u32[]{:S(2)}) %collective-permute-start.25) | collective-permute-done | bytes 1228832 | tf_op jit(solution)/shard_map/ppermute | solution.py:547
  430.1 11.3 %shard_map.187 = (bf16[2,1024,3200]{2,1,0:T(8,128)(2,1)}, bf16[2,1024,3200]{2,1,0:T(8,128)(2,1)}, bf16[2,5,640,1024]{3,2,1,0:T(8,128)(2,1)}, f32[2,1024,3200]{2,...) custom-call(f32[8,128]{1,0:T(8,128)} %get-tuple-element.124.refs_0_,, ...), custom_call_target="tpu_custom_call", output_to_operand_aliasing={{0}: (12, {}), {1}: (13, {}), {2}: (14, {}), {3}: (15, {}),... | custom-call | flops 491520000 | bytes 27033600 | tf_op jit(solution)/shard_map/pallas_call | solution.py:493
  441.4 1.0 copy-done.3
  442.5 6.6 %shard_map.188 = (bf16[2,1024,3200]{2,1,0:T(8,128)(2,1)}, bf16[2,1024,3200]{2,1,0:T(8,128)(2,1)}, bf16[2,5,640,1024]{3,2,1,0:T(8,128)(2,1)}, f32[2,1024,3200]{2,...) custom-call(f32[8,128]{1,0:T(8,128)} %get-tuple-element.124.refs_0_,, ...), custom_call_target="tpu_custom_call", output_to_operand_aliasing={{0}: (11, {}), {1}: (12, {}), {2}: (13, {}), {3}: (14, {}),... | custom-call | flops 245760000 | bytes 13516800 | tf_op jit(solution)/shard_map/pallas_call | solution.py:493
  (51 shorter events, 10.0 us)
Async XLA Ops:
  231.0 47.4 %collective-permute-start.4 = (bf16[3,64,3200]{2,1,0:T(8,128)(2,1)}, bf16[3,64,3200]{2,1,0:T(8,128)(2,1)S(1)}, u32[]{:S(2)}, u32[]{:S(2)}) collective-permute-start(bf16[3,64,3200]{2,1,0:T(8,128)(2,1)} %get-tuple-element.125.refs_1_), channel_id=1, source_target_pairs={{0,2},{1,3},{2,0},{3,1},{4,6},{5,7},{6,4},{7,5},{8,10},{9,11},{10,... | collective-permute-start | bytes 3686408 | tf_op jit(solution)/shard_map/ppermute | solution.py:540
  233.2 45.2 %collective-permute-start.5 = (bf16[3,64,3200]{2,1,0:T(8,128)(2,1)}, bf16[3,64,3200]{2,1,0:T(8,128)(2,1)}, u32[]{:S(2)}, u32[]{:S(2)}) collective-permute-start(bf16[3,64,3200]{2,1,0:T(8,128)(2,1)} %get-tuple-element.125.refs_1_), channel_id=1, source_target_pairs={{0,6},{1,7},{2,4},{3,5},{4,2},{5,3},{6,0},{7,1},{8,14},{9,15},{10,... | collective-permute-start | bytes 3686408 | tf_op jit(solution)/shard_map/ppermute | solution.py:541
  235.0 52.5 %collective-permute-start.6 = (bf16[3,64,3200]{2,1,0:T(8,128)(2,1)}, bf16[3,64,3200]{2,1,0:T(8,128)(2,1)}, u32[]{:S(2)}, u32[]{:S(2)}) collective-permute-start(bf16[3,64,3200]{2,1,0:T(8,128)(2,1)} %get-tuple-element.126.refs_2_), channel_id=1, source_target_pairs={{0,2},{1,3},{2,0},{3,1},{4,6},{5,7},{6,4},{7,5},{8,10},{9,11},{10,... | collective-permute-start | bytes 3686408 | tf_op jit(solution)/shard_map/ppermute | solution.py:540
  236.7 63.7 %collective-permute-start.7 = (bf16[3,64,3200]{2,1,0:T(8,128)(2,1)}, bf16[3,64,3200]{2,1,0:T(8,128)(2,1)}, u32[]{:S(2)}, u32[]{:S(2)}) collective-permute-start(bf16[3,64,3200]{2,1,0:T(8,128)(2,1)} %get-tuple-element.126.refs_2_), channel_id=1, source_target_pairs={{0,6},{1,7},{2,4},{3,5},{4,2},{5,3},{6,0},{7,1},{8,14},{9,15},{10,... | collective-permute-start | bytes 3686408 | tf_op jit(solution)/shard_map/ppermute | solution.py:541
  238.5 74.5 %collective-permute-start.10 = (bf16[3,64,3200]{2,1,0:T(8,128)(2,1)}, bf16[3,64,3200]{2,1,0:T(8,128)(2,1)}, u32[]{:S(2)}, u32[]{:S(2)}) collective-permute-start(bf16[3,64,3200]{2,1,0:T(8,128)(2,1)} %get-tuple-element.127.refs_3_), channel_id=1, source_target_pairs={{0,2},{1,3},{2,0},{3,1},{4,6},{5,7},{6,4},{7,5},{8,10},{9,11},{10,... | collective-permute-start | bytes 3686408 | tf_op jit(solution)/shard_map/ppermute | solution.py:540
  278.4 34.6 %collective-permute-start.9 = (bf16[3,64,3200]{2,1,0:T(8,128)(2,1)}, bf16[3,64,3200]{2,1,0:T(8,128)(2,1)}, u32[]{:S(2)}, u32[]{:S(2)}) collective-permute-start(bf16[3,64,3200]{2,1,0:T(8,128)(2,1)} %collective-permute-done.5.refs_2_), channel_id=1, source_target_pairs={{0,1},{1,0},{2,3},{3,2},{4,5},{5,4},{6,7},{7,6},{8,9},{9,8},{10,11... | collective-permute-start | bytes 3686408 | tf_op jit(solution)/shard_map/ppermute | solution.py:548
  278.5 35.4 %collective-permute-start.8 = (bf16[3,64,3200]{2,1,0:T(8,128)(2,1)S(1)}, bf16[3,64,3200]{2,1,0:T(8,128)(2,1)}, u32[]{:S(2)}, u32[]{:S(2)}) collective-permute-start(bf16[3,64,3200]{2,1,0:T(8,128)(2,1)S(1)} %collective-permute-done.4.refs_1_), channel_id=1, source_target_pairs={{0,1},{1,0},{2,3},{3,2},{4,5},{5,4},{6,7},{7,6},{8,9},{9,8},{10,11... | collective-permute-start | bytes 3686408 | tf_op jit(solution)/shard_map/ppermute | solution.py:548
  287.5 48.6 %collective-permute-start.11 = (bf16[3,64,3200]{2,1,0:T(8,128)(2,1)}, bf16[3,64,3200]{2,1,0:T(8,128)(2,1)}, u32[]{:S(2)}, u32[]{:S(2)}) collective-permute-start(bf16[3,64,3200]{2,1,0:T(8,128)(2,1)} %get-tuple-element.127.refs_3_), channel_id=1, source_target_pairs={{0,6},{1,7},{2,4},{3,5},{4,2},{5,3},{6,0},{7,1},{8,14},{9,15},{10,... | collective-permute-start | bytes 3686408 | tf_op jit(solution)/shard_map/ppermute | solution.py:541
  300.4 35.8 %collective-permute-start.12 = (bf16[3,64,3200]{2,1,0:T(8,128)(2,1)}, bf16[3,64,3200]{2,1,0:T(8,128)(2,1)}, u32[]{:S(2)}, u32[]{:S(2)}) collective-permute-start(bf16[3,64,3200]{2,1,0:T(8,128)(2,1)} %collective-permute-done.6.refs_1_), channel_id=1, source_target_pairs={{0,1},{1,0},{2,3},{3,2},{4,5},{5,4},{6,7},{7,6},{8,9},{9,8},{10,11... | collective-permute-start | bytes 3686408 | tf_op jit(solution)/shard_map/ppermute | solution.py:548
  313.0 23.7 %collective-permute-start.13 = (bf16[3,64,3200]{2,1,0:T(8,128)(2,1)}, bf16[3,64,3200]{2,1,0:T(8,128)(2,1)}, u32[]{:S(2)}, u32[]{:S(2)}) collective-permute-start(bf16[3,64,3200]{2,1,0:T(8,128)(2,1)} %collective-permute-done.7.refs_2_), channel_id=1, source_target_pairs={{0,1},{1,0},{2,3},{3,2},{4,5},{5,4},{6,7},{7,6},{8,9},{9,8},{10,11... | collective-permute-start | bytes 3686408 | tf_op jit(solution)/shard_map/ppermute | solution.py:548
  313.0 44.9 %collective-permute-start.14 = (bf16[3,64,3200]{2,1,0:T(8,128)(2,1)}, bf16[3,64,3200]{2,1,0:T(8,128)(2,1)}, u32[]{:S(2)}, u32[]{:S(2)}) collective-permute-start(bf16[3,64,3200]{2,1,0:T(8,128)(2,1)} %get-tuple-element.128.refs_4_), channel_id=1, source_target_pairs={{0,2},{1,3},{2,0},{3,1},{4,6},{5,7},{6,4},{7,5},{8,10},{9,11},{10,... | collective-permute-start | bytes 3686408 | tf_op jit(solution)/shard_map/ppermute | solution.py:540
  313.9 44.1 %collective-permute-start.15 = (bf16[3,64,3200]{2,1,0:T(8,128)(2,1)}, bf16[3,64,3200]{2,1,0:T(8,128)(2,1)}, u32[]{:S(2)}, u32[]{:S(2)}) collective-permute-start(bf16[3,64,3200]{2,1,0:T(8,128)(2,1)} %get-tuple-element.128.refs_4_), channel_id=1, source_target_pairs={{0,6},{1,7},{2,4},{3,5},{4,2},{5,3},{6,0},{7,1},{8,14},{9,15},{10,... | collective-permute-start | bytes 3686408 | tf_op jit(solution)/shard_map/ppermute | solution.py:541
  336.1 22.4 %collective-permute-start.18 = (bf16[3,64,3200]{2,1,0:T(8,128)(2,1)}, bf16[3,64,3200]{2,1,0:T(8,128)(2,1)}, u32[]{:S(2)}, u32[]{:S(2)}) collective-permute-start(bf16[3,64,3200]{2,1,0:T(8,128)(2,1)} %collective-permute-done.10.refs_1_), channel_id=1, source_target_pairs={{0,1},{1,0},{2,3},{3,2},{4,5},{5,4},{6,7},{7,6},{8,9},{9,8},{10,11... | collective-permute-start | bytes 3686408 | tf_op jit(solution)/shard_map/ppermute | solution.py:548
  336.2 23.9 %collective-permute-start.19 = (bf16[3,64,3200]{2,1,0:T(8,128)(2,1)}, bf16[3,64,3200]{2,1,0:T(8,128)(2,1)}, u32[]{:S(2)}, u32[]{:S(2)}) collective-permute-start(bf16[3,64,3200]{2,1,0:T(8,128)(2,1)} %collective-permute-done.11.refs_2_), channel_id=1, source_target_pairs={{0,1},{1,0},{2,3},{3,2},{4,5},{5,4},{6,7},{7,6},{8,9},{9,8},{10,11... | collective-permute-start | bytes 3686408 | tf_op jit(solution)/shard_map/ppermute | solution.py:548
  336.7 45.1 %collective-permute-start.20 = (bf16[3,64,3200]{2,1,0:T(8,128)(2,1)}, bf16[3,64,3200]{2,1,0:T(8,128)(2,1)}, u32[]{:S(2)}, u32[]{:S(2)}) collective-permute-start(bf16[3,64,3200]{2,1,0:T(8,128)(2,1)} %collective-permute-done.5.refs_2_), channel_id=1, source_target_pairs={{0,2},{1,3},{2,0},{3,1},{4,6},{5,7},{6,4},{7,5},{8,10},{9,11},{10,... | collective-permute-start | bytes 3686408 | tf_op jit(solution)/shard_map/ppermute | solution.py:547
  357.9 24.0 %collective-permute-start.16 = (bf16[3,64,3200]{2,1,0:T(8,128)(2,1)}, bf16[3,64,3200]{2,1,0:T(8,128)(2,1)S(1)}, u32[]{:S(2)}, u32[]{:S(2)}) collective-permute-start(bf16[3,64,3200]{2,1,0:T(8,128)(2,1)} %collective-permute-done.14.refs_1_), channel_id=1, source_target_pairs={{0,1},{1,0},{2,3},{3,2},{4,5},{5,4},{6,7},{7,6},{8,9},{9,8},{10,11... | collective-permute-start | bytes 3686408 | tf_op jit(solution)/shard_map/ppermute | solution.py:548
  358.0 23.9 %collective-permute-start.17 = (bf16[3,64,3200]{2,1,0:T(8,128)(2,1)}, bf16[3,64,3200]{2,1,0:T(8,128)(2,1)}, u32[]{:S(2)}, u32[]{:S(2)}) collective-permute-start(bf16[3,64,3200]{2,1,0:T(8,128)(2,1)} %collective-permute-done.15.refs_2_), channel_id=1, source_target_pairs={{0,1},{1,0},{2,3},{3,2},{4,5},{5,4},{6,7},{7,6},{8,9},{9,8},{10,11... | collective-permute-start | bytes 3686408 | tf_op jit(solution)/shard_map/ppermute | solution.py:548
  358.5 40.3 %collective-permute-start.21 = (bf16[3,64,3200]{2,1,0:T(8,128)(2,1)}, bf16[3,64,3200]{2,1,0:T(8,128)(2,1)}, u32[]{:S(2)}, u32[]{:S(2)}) collective-permute-start(bf16[3,64,3200]{2,1,0:T(8,128)(2,1)} %collective-permute-done.6.refs_1_), channel_id=1, source_target_pairs={{0,6},{1,7},{2,4},{3,5},{4,2},{5,3},{6,0},{7,1},{8,14},{9,15},{10,... | collective-permute-start | bytes 3686408 | tf_op jit(solution)/shard_map/ppermute | solution.py:547
  360.1 52.0 %collective-permute-start.24 = (bf16[3,64,3200]{2,1,0:T(8,128)(2,1)}, bf16[3,64,3200]{2,1,0:T(8,128)(2,1)}, u32[]{:S(2)}, u32[]{:S(2)}) collective-permute-start(bf16[3,64,3200]{2,1,0:T(8,128)(2,1)} %collective-permute-done.11.refs_2_), channel_id=1, source_target_pairs={{0,2},{1,3},{2,0},{3,1},{4,6},{5,7},{6,4},{7,5},{8,10},{9,11},{10,... | collective-permute-start | bytes 3686408 | tf_op jit(solution)/shard_map/ppermute | solution.py:547
  381.8 19.0 %collective-permute-start.23 = (bf16[3,64,3200]{2,1,0:T(8,128)(2,1)}, bf16[3,64,3200]{2,1,0:T(8,128)(2,1)}, u32[]{:S(2)}, u32[]{:S(2)}) collective-permute-start(bf16[3,64,3200]{2,1,0:T(8,128)(2,1)} %collective-permute-done.20.refs_3_), channel_id=1, source_target_pairs={{0,1},{1,0},{2,3},{3,2},{4,5},{5,4},{6,7},{7,6},{8,9},{9,8},{10,11... | collective-permute-start | bytes 3686408 | tf_op jit(solution)/shard_map/ppermute | solution.py:553
  398.8 13.4 %collective-permute-start.22 = (bf16[3,64,3200]{2,1,0:T(8,128)(2,1)}, bf16[3,64,3200]{2,1,0:T(8,128)(2,1)S(1)}, u32[]{:S(2)}, u32[]{:S(2)}) collective-permute-start(bf16[3,64,3200]{2,1,0:T(8,128)(2,1)} %collective-permute-done.21.refs_2_), channel_id=1, source_target_pairs={{0,1},{1,0},{2,3},{3,2},{4,5},{5,4},{6,7},{7,6},{8,9},{9,8},{10,11... | collective-permute-start | bytes 3686408 | tf_op jit(solution)/shard_map/ppermute | solution.py:553
  399.5 30.5 %collective-permute-start.25 = (bf16[3,64,3200]{2,1,0:T(8,128)(2,1)}, bf16[3,64,3200]{2,1,0:T(8,128)(2,1)}, u32[]{:S(2)}, u32[]{:S(2)}) collective-permute-start(bf16[3,64,3200]{2,1,0:T(8,128)(2,1)} %collective-permute-done.14.refs_1_), channel_id=1, source_target_pairs={{0,6},{1,7},{2,4},{3,5},{4,2},{5,3},{6,0},{7,1},{8,14},{9,15},{10,... | collective-permute-start | bytes 3686408 | tf_op jit(solution)/shard_map/ppermute | solution.py:547
  412.1 17.9 %collective-permute-start.27 = (bf16[3,64,3200]{2,1,0:T(8,128)(2,1)}, bf16[3,64,3200]{2,1,0:T(8,128)(2,1)}, u32[]{:S(2)}, u32[]{:S(2)}) collective-permute-start(bf16[3,64,3200]{2,1,0:T(8,128)(2,1)} %collective-permute-done.24.refs_2_), channel_id=1, source_target_pairs={{0,1},{1,0},{2,3},{3,2},{4,5},{5,4},{6,7},{7,6},{8,9},{9,8},{10,11... | collective-permute-start | bytes 3686408 | tf_op jit(solution)/shard_map/ppermute | solution.py:553
  430.1 11.4 %collective-permute-start.26 = (bf16[3,64,3200]{2,1,0:T(8,128)(2,1)}, bf16[3,64,3200]{2,1,0:T(8,128)(2,1)S(1)}, u32[]{:S(2)}, u32[]{:S(2)}) collective-permute-start(bf16[3,64,3200]{2,1,0:T(8,128)(2,1)} %collective-permute-done.25.refs_2_), channel_id=1, source_target_pairs={{0,1},{1,0},{2,3},{3,2},{4,5},{5,4},{6,7},{7,6},{8,9},{9,8},{10,11... | collective-permute-start | bytes 3686408 | tf_op jit(solution)/shard_map/ppermute | solution.py:553
  (8 other events, 36.3 us)

commit v3 on v2

--- a/solution.py
+++ b/solution.py
@@ -8,7 +8,7 @@
 from jax.sharding import PartitionSpec as P
 
 
-SLOTS = 4
+SLOTS = 6
 
 
 MESH = pl.DeviceIdType.MESH
@@ -26,27 +26,30 @@
 def backward_kernel(
     n, layers, x_ref, dy_ref, wg_ref, wu_ref, wd_ref, *refs
 ):
-    outs, factor_ref, refs = refs[: 2 * layers], refs[2 * layers], refs[2 * layers + 1 :]
+    outs, besides, factor_ref, refs = refs[: 2 * layers], refs[2 * layers : 4 * layers], refs[4 * layers], refs[4 * layers + 1 :]
     (hs, a, aT, dh, wg, wu, wd, actT, dgate, dup, acc_g, acc_u, send0, own, rcv0, rcv1, rcv2, fin, squares, parts,
-     w_sem, h_sem, send0_sem, rcv0_sem, send1_sem, rcv1_sem, send2_sem, rcv2_sem, fin_sem, ssend_sem, srecv_sem,
+     w_sem, h_sem, send0_sem, rcv0_sem, send1_sem, rcv1_sem, send2_sem, rcv2_sem, fin_sem, bsend_sem, brecv_sem, ssend_sem, srecv_sem,
      credit_p, credit_a, credit_b) = refs
     me, c, x, xa, xb, xo = hops()
     peer, to_a, to_b = 2 * x + 1 - c, 2 * xa + c, 2 * xb + c
     tokens, depth = dh.shape
-    width = wg.shape[-1]
+    width, broad, hidden = dgate.shape[-1], wg.shape[-1], wg_ref.shape[-1]
+    many, rest = hidden // broad, hidden % broad
     steps = layers * TILES
     half = depth // 2
-    ahead = (layers - 1) * TILES
+    ahead = (layers - 1) * (many + 1)
     tall = 512
 
-    def weights_of(t, number):
-        j, slot = t % TILES, t % 2
-        at = pl.ds(pl.multiple_of(j * width, width), width)
+    def piece(t, number, start, size):
+        slot, at, here = t % 2, pl.ds(start, size), pl.ds(0, size)
         return [
-            pltpu.make_async_copy(wg_ref.at[number, :, at], wg.at[slot], w_sem.at[0, slot]),
-            pltpu.make_async_copy(wu_ref.at[number, :, at], wu.at[slot], w_sem.at[1, slot]),
-            pltpu.make_async_copy(wd_ref.at[number, at], wd.at[slot], w_sem.at[2, slot]),
+            pltpu.make_async_copy(wg_ref.at[number, :, at], wg.at[slot, :, here], w_sem.at[0, slot]),
+            pltpu.make_async_copy(wu_ref.at[number, :, at], wu.at[slot, :, here], w_sem.at[1, slot]),
+            pltpu.make_async_copy(wd_ref.at[number, at], wd.at[slot, here], w_sem.at[2, slot]),
         ]
+
+    def weights_of(s):
+        return piece(s + ahead, layers - 1 - s // TILES, pl.multiple_of(s % TILES * width, 128), width)
 
     def turn(source, target):
         @pl.loop(0, tokens // 128)
@@ -66,7 +69,7 @@
     first_h.start()
     first_dh = pltpu.make_async_copy(dy_ref, dh, h_sem.at[1])
     first_dh.start()
-    for one in weights_of(0, 0):
+    for one in piece(0, 0, 0, broad):
         one.start()
 
     barrier = pltpu.get_barrier_semaphore()
@@ -80,21 +83,41 @@
         norm(hs.at[number])
         acc_g[...] = jnp.zeros_like(acc_g)
 
-        @pl.loop(number * TILES, (number + 1) * TILES)
-        def _(t):
-            slot = t % 2
-            for one in weights_of(t, number):
-                one.wait()
-            for one in weights_of(t + 1, (t + 1) // TILES):
-                one.start()
+        base = number * (many + 1)
+
+        def onward(slot, size):
+            here = pl.ds(0, size)
 
             @pl.loop(0, tokens // tall)
             def _(r):
                 at = pl.ds(pl.multiple_of(r * tall, tall), tall)
-                gate = jnp.dot(a[at], wg[slot], preferred_element_type=jnp.float32)
-                up = jnp.dot(a[at], wu[slot], preferred_element_type=jnp.float32)
-                dup[at] = (gate * jax.nn.sigmoid(gate) * up).astype(jnp.bfloat16)
-                acc_g[at] += jnp.dot(dup[at], wd[slot], preferred_element_type=jnp.float32)
+                gate = jnp.dot(a[at], wg[slot, :, here], preferred_element_type=jnp.float32)
+                up = jnp.dot(a[at], wu[slot, :, here], preferred_element_type=jnp.float32)
+                hot = (gate * jax.nn.sigmoid(gate) * up).astype(jnp.bfloat16)
+                acc_g[at] += jnp.dot(hot, wd[slot, here], preferred_element_type=jnp.float32)
+
+        @pl.loop(0, many)
+        def _(i):
+            for one in piece(base + i, number, pl.multiple_of(i * broad, 128), broad):
+                one.wait()
+
+            @pl.when(i + 1 < many)
+            def _():
+                for one in piece(base + i + 1, number, pl.multiple_of((i + 1) * broad, 128), broad):
+                    one.start()
+
+            @pl.when(i + 1 == many)
+            def _():
+                for one in piece(base + many, number, many * broad, rest):
+                    one.start()
+
+            onward((base + i) % 2, broad)
+
+        for one in piece(base + many, number, many * broad, rest):
+            one.wait()
+        for one in weights_of(0) if number == layers - 2 else piece(base + many + 1, number + 1, 0, broad):
+            one.start()
+        onward((base + many) % 2, rest)
 
         @pl.loop(0, tokens // 64)
         def _(r):
@@ -164,6 +187,13 @@
         at = pl.ds(pl.multiple_of((s % TILES) * width, width), width)
         return [pltpu.make_async_copy(fin.at[colour], outs[2 * number + colour].at[:, :, at], fin_sem.at[colour]) for colour in range(2)]
 
+    def over(s, number):
+        at = pl.ds(pl.multiple_of((s % TILES) * width, width), width)
+        return [
+            remote(fin.at[colour], besides[2 * number + colour].at[:, :, at], bsend_sem.at[colour], brecv_sem.at[s, colour], peer)
+            for colour in range(2)
+        ]
+
     def finish(s):
         for *_, one in step_two(s):
             one.wait_recv()
@@ -172,6 +202,8 @@
         def _():
             for one in fin_copies(s, 0):
                 one.wait()
+            for one in over(s, 0):
+                one.wait_send()
 
         for colour in range(2):
             for mat, at, total in summed(s, 2 * x + colour, ((rcv1, 2 * colour), (rcv2, colour))):
@@ -182,7 +214,7 @@
 
             @pl.when(layers - 1 - s // TILES == number)
             def _():
-                for one in fin_copies(s, number):
+                for one in fin_copies(s, number) + over(s, number):
                     one.start()
 
         for _, one in step_one(s):
@@ -222,22 +254,22 @@
 
     @pl.loop(0, steps)
     def _(s):
-        t, even, k = s + ahead, s % 2, s % DEEP
-        slot = t % 2
-        for one in weights_of(t, layers - 1 - s // TILES):
+        slot, even, k = (s + ahead) % 2, s % 2, s % DEEP
+        here = pl.ds(0, width)
+        for one in weights_of(s):
             one.wait()
 
         @pl.when(s + 1 < steps)
         def _():
-            for one in weights_of(t + 1, layers - 1 - (s + 1) // TILES):
+            for one in weights_of(s + 1):
                 one.start()
 
         @pl.loop(0, tokens // tall)
         def _(r):
             at = pl.ds(pl.multiple_of(r * tall, tall), tall)
-            gate = jnp.dot(a[at], wg[slot], preferred_element_type=jnp.float32)
-            up = jnp.dot(a[at], wu[slot], preferred_element_type=jnp.float32)
-            by_act = lax.dot_general(dh[at], wd[slot], (((1,), (1,)), ((), ())), preferred_element_type=jnp.float32)
+            gate = jnp.dot(a[at], wg[slot, :, here], preferred_element_type=jnp.float32)
+            up = jnp.dot(a[at], wu[slot, :, here], preferred_element_type=jnp.float32)
+            by_act = lax.dot_general(dh[at], wd[slot, here], (((1,), (1,)), ((), ())), preferred_element_type=jnp.float32)
             by_act = by_act.astype(jnp.bfloat16).astype(jnp.float32)
             share = jax.nn.sigmoid(gate)
             silu = gate * share
@@ -285,7 +317,7 @@
             def _(r):
                 at = pl.ds(pl.multiple_of(r * tall, tall), tall)
                 for total, by, w in ((acc_g, dgate, wg), (acc_u, dup, wu)):
-                    total[at] += lax.dot_general(by[at], w[slot], (((1,), (1,)), ((), ())), preferred_element_type=jnp.float32)
+                    total[at] += lax.dot_general(by[at], w[slot, :, here], (((1,), (1,)), ((), ())), preferred_element_type=jnp.float32)
 
             @pl.when(s % TILES == TILES - 1)
             def _():
@@ -307,6 +339,8 @@
         finish(jnp.int32(steps - back))
     for one in fin_copies(jnp.int32(steps - 1), 0):
         one.wait()
+    for one in over(jnp.int32(steps - 1), 0):
+        one.wait_send()
     swap(jnp.int32(steps - 2)).wait_send()
     swap(jnp.int32(steps - 1)).wait_send()
 
@@ -317,6 +351,9 @@
 
     for k in range(1, n):
         share(k).start()
+    for s in range(steps):
+        for one in over(s, layers - 1 - s // TILES):
+            one.wait_recv()
     for k in range(1, n):
         share(k).wait()
     total = parts[0]
@@ -329,22 +366,23 @@
 def backward(n, x, dy, weights):
     layers, depth, hidden = weights[0].shape
     tokens, width, rows = dy.shape[0], hidden // TILES, depth // 16
+    broad = (width // 256 + 1) * 256
     bf16, dma, regular = jnp.bfloat16, pltpu.SemaphoreType.DMA, pltpu.SemaphoreType.REGULAR
     any_spec = pl.BlockSpec(memory_space=pl.ANY)
     out = pl.pallas_call(
         functools.partial(backward_kernel, n, layers),
-        out_shape=[jax.ShapeDtypeStruct((3, rows, hidden), bf16)] * (2 * layers)
+        out_shape=[jax.ShapeDtypeStruct((3, rows, hidden), bf16)] * (4 * layers)
         + [jax.ShapeDtypeStruct((8, 128), jnp.float32)],
         in_specs=[any_spec] * 5,
-        out_specs=[any_spec] * (2 * layers) + [pl.BlockSpec(memory_space=pltpu.VMEM)],
+        out_specs=[any_spec] * (4 * layers) + [pl.BlockSpec(memory_space=pltpu.VMEM)],
         scratch_shapes=[
             pltpu.VMEM((layers, tokens, depth), bf16),
             pltpu.VMEM((tokens, depth), bf16),
             pltpu.VMEM((depth, tokens), bf16),
             pltpu.VMEM((tokens, depth), bf16),
-            pltpu.VMEM((2, depth, width), bf16),
-            pltpu.VMEM((2, depth, width), bf16),
-            pltpu.VMEM((2, width, depth), bf16),
+            pltpu.VMEM((2, depth, broad), bf16),
+            pltpu.VMEM((2, depth, broad), bf16),
+            pltpu.VMEM((2, broad, depth), bf16),
             pltpu.VMEM((width, tokens), bf16),
             pltpu.VMEM((tokens, width), bf16),
             pltpu.VMEM((tokens, width), bf16),
@@ -367,6 +405,8 @@
             dma((DEEP, 2)),
             dma((DEEP, 2)),
             dma((2,)),
+            dma((2,)),
+            dma((layers * TILES, 2)),
             dma((n,)),
             dma((n,)),
             regular,
@@ -376,7 +416,7 @@
         compiler_params=pltpu.CompilerParams(collective_id=0, has_side_effects=True, vmem_limit_bytes=67_043_328),
         cost_estimate=pl.CostEstimate(flops=16 * tokens * depth * hidden * layers, bytes_accessed=2**27, transcendentals=0),
     )(x, dy, *weights)
-    return out[:-1], out[-1]
+    return out[: 2 * layers], out[2 * layers : -1], out[-1]
 
 
 def update_kernel(items, n_new, *refs):
@@ -517,7 +557,7 @@
     peers = [(i, i ^ 1) for i in range(n)]
     to_a, to_b, to_peer = (functools.partial(lax.ppermute, axis_name="dp", perm=perm) for perm in (pair_a, pair_b, peers))
 
-    def gather(shards, factor, arrays):
+    def gather(shards, beside, factor, arrays):
         layers = arrays[0].shape[0]
         calls = []
 
@@ -539,19 +579,22 @@
         for _, _, own in shards:
             one = to_a(own)
             near.append((one, to_b(own)))
-        beside = [to_peer(own) for _, _, own in shards]
         new = run(None, [(u, own, 0, 0) for u, (_, _, own) in enumerate(shards)] + [(u, g, 1, 0) for u, g in enumerate(beside)])
         far, waiting = [], []
         for u, (_, colour, _) in enumerate(shards):
+            if u >= 2:
+                new, waiting = run(new, waiting), []
             new, got = after(new, near[u])
             far.append(to_b(got[0]) if colour else to_a(got[1]))
             across = [(u, to_peer(g), 1, 1 + j) for j, g in enumerate(got)]
             new = run(new, [(u, g, 0, 1 + j) for j, g in enumerate(got)] + waiting)
             waiting = across
-        for u, g in enumerate(far):
-            new, got = after(new, g)
-            across = [(u, to_peer(got), 1, 3)]
-            new = run(new, waiting + [(u, got, 0, 3)])
+        for u in range(0, len(far), 2):
+            new = run(new, waiting)
+            new, got = after(new, far[u : u + 2])
+            got = list(enumerate(got, u))
+            across = [(i, to_peer(g), 1, 3) for i, g in got]
+            new = run(new, [(i, g, 0, 3) for i, g in got])
             waiting = across
         new = run(new, waiting)
         return new
@@ -559,10 +602,14 @@
     def step(x, dy, *arrays):
         weights = arrays[:3]
         layers = weights[0].shape[0]
-        blocks, factor = backward(n, x[0], dy[0], weights)
-        shards = [(number, colour, blocks[2 * number + colour]) for number in reversed(range(layers)) for colour in range(2)]
-
-        new = gather(shards, factor, arrays)
+        blocks, besides, factor = backward(n, x[0], dy[0], weights)
+        shards, beside = [], []
+        for number in reversed(range(layers)):
+            for colour in range(2):
+                shards.append((number, colour, blocks[2 * number + colour]))
+                beside.append(besides[2 * number + colour])
+
+        new = gather(shards, beside, factor, arrays)
         new = [o.reshape(o.shape[0], -1, o.shape[-1]) for o in new]
         return tuple(new)
 

time: 450 us -> 435 us (0.967)
  Pallas kernels: 398 us -> 391 us
  waiting for transfers between devices: 29.2 us -> 22.7 us
    ppermute x4, waiting for transfers between devices: 21.1 us -> 6.72 us  [gather(): one = to_a(own)]
    ppermute x4, waiting for transfers between devices: 5.38 us -> 12.6 us  [gather(): far.append(to_b(got[0]) if colour else to_a(got[1]))]
    pallas_call x10 -> x12, Pallas kernels: 169 us -> 164 us  [update(): pl.pallas_call(functools.partial(update_kernel, items, new is None), out_...]
  transfers between devices with their start and end apart: 28 -> 24, of which waited for: 7 -> 8; matrix products, arithmetic and copies ran while one was open for 0% -> 0% of each run, Pallas kernels for 36% -> 35%
where the time goes in v3:
time: 435 us
  Pallas kernels  391 us (90%)
  waiting for transfers between devices  22.7 us (5%)
  starting transfers between devices  15.7 us (4%)
  local copies, waits for them, and re-layouts  4.62 us (1%)
    pallas_call x1, Pallas kernels, backward(): pl.pallas_call(functools.partial(backward_kernel, n, layers), out_shape=[...  227 us
    pallas_call x12, Pallas kernels, update(): pl.pallas_call(functools.partial(update_kernel, items, new is None), out_...  164 us
    ppermute x4, waiting for transfers between devices, gather(): far.append(to_b(got[0]) if colour else to_a(got[1]))  12.6 us
  transfers between devices with their start and end apart: 24, of which 8 were waited for; matrix products, arithmetic and copies ran while one was open for 0% of the time, Pallas kernels for 35%

profile of v3, /device:TPU:112, one launch (start us, length us, event | category | flops | bytes accessed | tf_op | source)
XLA Modules:
  0.0 434.9 jit_solution(10814181991246356386)
XLA Ops:
  0.6 227.0 %shard_map.178 = (bf16[3,64,3200]{2,1,0:T(8,128)(2,1)}, bf16[3,64,3200]{2,1,0:T(8,128)(2,1)}, bf16[3,64,3200]{2,1,0:T(8,128)(2,1)}, bf16[3,64,3200]{2,1,0:T(8,12...) custom-call(bf16[1024,1024]{1,0:T(8,128)(2,1)} %bitcast.47, ...), custom_call_target="tpu_custom_call" | custom-call | flops 107374182400 | bytes 134217728 | tf_op jit(solution)/shard_map/pallas_call | solution.py:372
  228.6 1.7 collective-permute-start.1
  230.8 1.6 collective-permute-start.3
  232.4 36.5 %shard_map.179 = (bf16[2,1024,3200]{2,1,0:T(8,128)(2,1)}, bf16[2,1024,3200]{2,1,0:T(8,128)(2,1)}, bf16[2,5,640,1024]{3,2,1,0:T(8,128)(2,1)}, f32[2,1024,3200]{2,...) custom-call(f32[8,128]{1,0:T(8,128)} %get-tuple-element.144.refs_0_,, ...), custom_call_target="tpu_custom_call" | custom-call | flops 1966080000 | bytes 108134400 | tf_op jit(solution)/shard_map/pallas_call | solution.py:533
  270.0 10.8 %shard_map.180 = (bf16[2,1024,3200]{2,1,0:T(8,128)(2,1)}, bf16[2,1024,3200]{2,1,0:T(8,128)(2,1)}, bf16[2,5,640,1024]{3,2,1,0:T(8,128)(2,1)}, f32[2,1024,3200]{2,...) custom-call(f32[8,128]{1,0:T(8,128)} %get-tuple-element.144.refs_0_,, ...), custom_call_target="tpu_custom_call", output_to_operand_aliasing={{0}: (12, {}), {1}: (13, {}), {2}: (14, {}), {3}: (15, {}),... | custom-call | flops 491520000 | bytes 27033600 | tf_op jit(solution)/shard_map/pallas_call | solution.py:533
  280.8 2.7 collective-permute-done.2.refs_1_
  283.5 1.8 collective-permute-done.3.refs_2_
  285.8 1.7 collective-permute-start.9
  287.5 19.4 %shard_map.181 = (bf16[2,1024,3200]{2,1,0:T(8,128)(2,1)}, bf16[2,1024,3200]{2,1,0:T(8,128)(2,1)}, bf16[2,5,640,1024]{3,2,1,0:T(8,128)(2,1)}, f32[2,1024,3200]{2,...) custom-call(f32[8,128]{1,0:T(8,128)} %get-tuple-element.144.refs_0_,, ...), custom_call_target="tpu_custom_call", output_to_operand_aliasing={{0}: (14, {}), {1}: (15, {}), {2}: (16, {}), {3}: (17, {}),... | custom-call | flops 983040000 | bytes 54067200 | tf_op jit(solution)/shard_map/pallas_call | solution.py:533
  306.8 10.9 %shard_map.182 = (bf16[2,1024,3200]{2,1,0:T(8,128)(2,1)}, bf16[2,1024,3200]{2,1,0:T(8,128)(2,1)}, bf16[2,5,640,1024]{3,2,1,0:T(8,128)(2,1)}, f32[2,1024,3200]{2,...) custom-call(f32[8,128]{1,0:T(8,128)} %get-tuple-element.144.refs_0_,, ...), custom_call_target="tpu_custom_call", output_to_operand_aliasing={{0}: (12, {}), {1}: (13, {}), {2}: (14, {}), {3}: (15, {}),... | custom-call | flops 491520000 | bytes 27033600 | tf_op jit(solution)/shard_map/pallas_call | solution.py:533
  318.9 2.0 collective-permute-start.13
  320.9 10.8 %shard_map.183 = (bf16[2,1024,3200]{2,1,0:T(8,128)(2,1)}, bf16[2,1024,3200]{2,1,0:T(8,128)(2,1)}, bf16[2,5,640,1024]{3,2,1,0:T(8,128)(2,1)}, f32[2,1024,3200]{2,...) custom-call(f32[8,128]{1,0:T(8,128)} %get-tuple-element.144.refs_0_,, ...), custom_call_target="tpu_custom_call", output_to_operand_aliasing={{0}: (12, {}), {1}: (13, {}), {2}: (14, {}), {3}: (15, {}),... | custom-call | flops 491520000 | bytes 27033600 | tf_op jit(solution)/shard_map/pallas_call | solution.py:533
  332.8 10.8 %shard_map.184 = (bf16[2,1024,3200]{2,1,0:T(8,128)(2,1)}, bf16[2,1024,3200]{2,1,0:T(8,128)(2,1)}, bf16[2,5,640,1024]{3,2,1,0:T(8,128)(2,1)}, f32[2,1024,3200]{2,...) custom-call(f32[8,128]{1,0:T(8,128)} %get-tuple-element.144.refs_0_,, ...), custom_call_target="tpu_custom_call", output_to_operand_aliasing={{0}: (12, {}), {1}: (13, {}), {2}: (14, {}), {3}: (15, {}),... | custom-call | flops 491520000 | bytes 27033600 | tf_op jit(solution)/shard_map/pallas_call | solution.py:533
  343.6 4.1 collective-permute-done.12.refs_1_
  347.7 1.5 collective-permute-done.13.refs_2_
  349.7 2.0 collective-permute-start.17
  351.7 10.8 %shard_map.185 = (bf16[2,1024,3200]{2,1,0:T(8,128)(2,1)}, bf16[2,1024,3200]{2,1,0:T(8,128)(2,1)}, bf16[2,5,640,1024]{3,2,1,0:T(8,128)(2,1)}, f32[2,1024,3200]{2,...) custom-call(f32[8,128]{1,0:T(8,128)} %get-tuple-element.144.refs_0_,, ...), custom_call_target="tpu_custom_call", output_to_operand_aliasing={{0}: (12, {}), {1}: (13, {}), {2}: (14, {}), {3}: (15, {}),... | custom-call | flops 491520000 | bytes 27033600 | tf_op jit(solution)/shard_map/pallas_call | solution.py:533
  363.5 10.8 %shard_map.186 = (bf16[2,1024,3200]{2,1,0:T(8,128)(2,1)}, bf16[2,1024,3200]{2,1,0:T(8,128)(2,1)}, bf16[2,5,640,1024]{3,2,1,0:T(8,128)(2,1)}, f32[2,1024,3200]{2,...) custom-call(f32[8,128]{1,0:T(8,128)} %get-tuple-element.144.refs_0_,, ...), custom_call_target="tpu_custom_call", output_to_operand_aliasing={{0}: (12, {}), {1}: (13, {}), {2}: (14, {}), {3}: (15, {}),... | custom-call | flops 491520000 | bytes 27033600 | tf_op jit(solution)/shard_map/pallas_call | solution.py:533
  374.3 5.9 %collective-permute-done.17.refs_2_ = bf16[3,64,3200]{2,1,0:T(8,128)(2,1)} collective-permute-done((bf16[3,64,3200]{2,1,0:T(8,128)(2,1)}, bf16[3,64,3200]{2,1,0:T(8,128)(2,1)}, u32[]{:S(2)}, u32[]{:S(2)}) %collective-permute-start.17) | collective-permute-done | bytes 1228832 | tf_op jit(solution)/shard_map/ppermute | solution.py:588
  382.7 10.8 %shard_map.187 = (bf16[2,1024,3200]{2,1,0:T(8,128)(2,1)}, bf16[2,1024,3200]{2,1,0:T(8,128)(2,1)}, bf16[2,5,640,1024]{3,2,1,0:T(8,128)(2,1)}, f32[2,1024,3200]{2,...) custom-call(f32[8,128]{1,0:T(8,128)} %get-tuple-element.144.refs_0_,, ...), custom_call_target="tpu_custom_call", output_to_operand_aliasing={{0}: (12, {}), {1}: (13, {}), {2}: (14, {}), {3}: (15, {}),... | custom-call | flops 491520000 | bytes 27033600 | tf_op jit(solution)/shard_map/pallas_call | solution.py:533
  394.5 10.8 %shard_map.188 = (bf16[2,1024,3200]{2,1,0:T(8,128)(2,1)}, bf16[2,1024,3200]{2,1,0:T(8,128)(2,1)}, bf16[2,5,640,1024]{3,2,1,0:T(8,128)(2,1)}, f32[2,1024,3200]{2,...) custom-call(f32[8,128]{1,0:T(8,128)} %get-tuple-element.144.refs_0_,, ...), custom_call_target="tpu_custom_call", output_to_operand_aliasing={{0}: (12, {}), {1}: (13, {}), {2}: (14, {}), {3}: (15, {}),... | custom-call | flops 491520000 | bytes 27033600 | tf_op jit(solution)/shard_map/pallas_call | solution.py:533
  405.3 5.1 %collective-permute-done.20.refs_1_ = bf16[3,64,3200]{2,1,0:T(8,128)(2,1)} collective-permute-done((bf16[3,64,3200]{2,1,0:T(8,128)(2,1)}, bf16[3,64,3200]{2,1,0:T(8,128)(2,1)}, u32[]{:S(2)}, u32[]{:S(2)}) %collective-permute-start.20) | collective-permute-done | bytes 1228832 | tf_op jit(solution)/shard_map/ppermute | solution.py:588
  412.1 10.8 %shard_map.189 = (bf16[2,1024,3200]{2,1,0:T(8,128)(2,1)}, bf16[2,1024,3200]{2,1,0:T(8,128)(2,1)}, bf16[2,5,640,1024]{3,2,1,0:T(8,128)(2,1)}, f32[2,1024,3200]{2,...) custom-call(f32[8,128]{1,0:T(8,128)} %get-tuple-element.144.refs_0_,, ...), custom_call_target="tpu_custom_call", output_to_operand_aliasing={{0}: (12, {}), {1}: (13, {}), {2}: (14, {}), {3}: (15, {}),... | custom-call | flops 491520000 | bytes 27033600 | tf_op jit(solution)/shard_map/pallas_call | solution.py:533
  424.0 10.8 %shard_map.190 = (bf16[2,1024,3200]{2,1,0:T(8,128)(2,1)}, bf16[2,1024,3200]{2,1,0:T(8,128)(2,1)}, bf16[2,5,640,1024]{3,2,1,0:T(8,128)(2,1)}, f32[2,1024,3200]{2,...) custom-call(f32[8,128]{1,0:T(8,128)} %get-tuple-element.144.refs_0_,, ...), custom_call_target="tpu_custom_call", output_to_operand_aliasing={{0}: (12, {}), {1}: (13, {}), {2}: (14, {}), {3}: (15, {}),... | custom-call | flops 491520000 | bytes 27033600 | tf_op jit(solution)/shard_map/pallas_call | solution.py:533
  (47 shorter events, 13.1 us)
Async XLA Ops:
  227.7 41.2 %collective-permute-start = (bf16[3,64,3200]{2,1,0:T(8,128)(2,1)}, bf16[3,64,3200]{2,1,0:T(8,128)(2,1)S(1)}, u32[]{:S(2)}, u32[]{:S(2)}) collective-permute-start(bf16[3,64,3200]{2,1,0:T(8,128)(2,1)} %get-tuple-element.145.refs_1_), channel_id=1, source_target_pairs={{0,2},{1,3},{2,0},{3,1},{4,6},{5,7},{6,4},{7,5},{8,10},{9,11},{10,... | collective-permute-start | bytes 3686408 | tf_op jit(solution)/shard_map/ppermute | solution.py:580
  228.6 40.3 %collective-permute-start.1 = (bf16[3,64,3200]{2,1,0:T(8,128)(2,1)}, bf16[3,64,3200]{2,1,0:T(8,128)(2,1)}, u32[]{:S(2)}, u32[]{:S(2)}) collective-permute-start(bf16[3,64,3200]{2,1,0:T(8,128)(2,1)} %get-tuple-element.145.refs_1_), channel_id=1, source_target_pairs={{0,6},{1,7},{2,4},{3,5},{4,2},{5,3},{6,0},{7,1},{8,14},{9,15},{10,... | collective-permute-start | bytes 3686408 | tf_op jit(solution)/shard_map/ppermute | solution.py:581
  230.3 53.1 %collective-permute-start.2 = (bf16[3,64,3200]{2,1,0:T(8,128)(2,1)}, bf16[3,64,3200]{2,1,0:T(8,128)(2,1)}, u32[]{:S(2)}, u32[]{:S(2)}) collective-permute-start(bf16[3,64,3200]{2,1,0:T(8,128)(2,1)} %get-tuple-element.146.refs_2_), channel_id=1, source_target_pairs={{0,2},{1,3},{2,0},{3,1},{4,6},{5,7},{6,4},{7,5},{8,10},{9,11},{10,... | collective-permute-start | bytes 3686408 | tf_op jit(solution)/shard_map/ppermute | solution.py:580
  230.8 54.5 %collective-permute-start.3 = (bf16[3,64,3200]{2,1,0:T(8,128)(2,1)}, bf16[3,64,3200]{2,1,0:T(8,128)(2,1)}, u32[]{:S(2)}, u32[]{:S(2)}) collective-permute-start(bf16[3,64,3200]{2,1,0:T(8,128)(2,1)} %get-tuple-element.146.refs_2_), channel_id=1, source_target_pairs={{0,6},{1,7},{2,4},{3,5},{4,2},{5,3},{6,0},{7,1},{8,14},{9,15},{10,... | collective-permute-start | bytes 3686408 | tf_op jit(solution)/shard_map/ppermute | solution.py:581
  269.0 16.8 %collective-permute-start.7 = (bf16[3,64,3200]{2,1,0:T(8,128)(2,1)}, bf16[3,64,3200]{2,1,0:T(8,128)(2,1)}, u32[]{:S(2)}, u32[]{:S(2)}) collective-permute-start(bf16[3,64,3200]{2,1,0:T(8,128)(2,1)} %collective-permute-done.1.refs_2_), channel_id=1, source_target_pairs={{0,1},{1,0},{2,3},{3,2},{4,5},{5,4},{6,7},{7,6},{8,9},{9,8},{10,11... | collective-permute-start | bytes 3686408 | tf_op jit(solution)/shard_map/ppermute | solution.py:589
  269.1 18.4 %collective-permute-start.6 = (bf16[3,64,3200]{2,1,0:T(8,128)(2,1)S(1)}, bf16[3,64,3200]{2,1,0:T(8,128)(2,1)}, u32[]{:S(2)}, u32[]{:S(2)}) collective-permute-start(bf16[3,64,3200]{2,1,0:T(8,128)(2,1)S(1)} %collective-permute-done.refs_1_), channel_id=1, source_target_pairs={{0,1},{1,0},{2,3},{3,2},{4,5},{5,4},{6,7},{7,6},{8,9},{9,8},{10,11... | collective-permute-start | bytes 3686408 | tf_op jit(solution)/shard_map/ppermute | solution.py:589
  285.2 21.6 %collective-permute-start.4 = (bf16[3,64,3200]{2,1,0:T(8,128)(2,1)}, bf16[3,64,3200]{2,1,0:T(8,128)(2,1)}, u32[]{:S(2)}, u32[]{:S(2)}) collective-permute-start(bf16[3,64,3200]{2,1,0:T(8,128)(2,1)} %collective-permute-done.2.refs_1_), channel_id=1, source_target_pairs={{0,1},{1,0},{2,3},{3,2},{4,5},{5,4},{6,7},{7,6},{8,9},{9,8},{10,11... | collective-permute-start | bytes 3686408 | tf_op jit(solution)/shard_map/ppermute | solution.py:589
  285.2 21.6 %collective-permute-start.5 = (bf16[3,64,3200]{2,1,0:T(8,128)(2,1)}, bf16[3,64,3200]{2,1,0:T(8,128)(2,1)}, u32[]{:S(2)}, u32[]{:S(2)}) collective-permute-start(bf16[3,64,3200]{2,1,0:T(8,128)(2,1)} %collective-permute-done.3.refs_2_), channel_id=1, source_target_pairs={{0,1},{1,0},{2,3},{3,2},{4,5},{5,4},{6,7},{7,6},{8,9},{9,8},{10,11... | collective-permute-start | bytes 3686408 | tf_op jit(solution)/shard_map/ppermute | solution.py:589
  285.7 32.0 %collective-permute-start.8 = (bf16[3,64,3200]{2,1,0:T(8,128)(2,1)}, bf16[3,64,3200]{2,1,0:T(8,128)(2,1)}, u32[]{:S(2)}, u32[]{:S(2)}) collective-permute-start(bf16[3,64,3200]{2,1,0:T(8,128)(2,1)} %get-tuple-element.147.refs_3_), channel_id=1, source_target_pairs={{0,2},{1,3},{2,0},{3,1},{4,6},{5,7},{6,4},{7,5},{8,10},{9,11},{10,... | collective-permute-start | bytes 3686408 | tf_op jit(solution)/shard_map/ppermute | solution.py:580
  285.8 32.0 %collective-permute-start.9 = (bf16[3,64,3200]{2,1,0:T(8,128)(2,1)}, bf16[3,64,3200]{2,1,0:T(8,128)(2,1)}, u32[]{:S(2)}, u32[]{:S(2)}) collective-permute-start(bf16[3,64,3200]{2,1,0:T(8,128)(2,1)} %get-tuple-element.147.refs_3_), channel_id=1, source_target_pairs={{0,6},{1,7},{2,4},{3,5},{4,2},{5,3},{6,0},{7,1},{8,14},{9,15},{10,... | collective-permute-start | bytes 3686408 | tf_op jit(solution)/shard_map/ppermute | solution.py:581
  317.7 13.9 %collective-permute-start.10 = (bf16[3,64,3200]{2,1,0:T(8,128)(2,1)}, bf16[3,64,3200]{2,1,0:T(8,128)(2,1)S(1)}, u32[]{:S(2)}, u32[]{:S(2)}) collective-permute-start(bf16[3,64,3200]{2,1,0:T(8,128)(2,1)} %collective-permute-done.8.refs_1_), channel_id=1, source_target_pairs={{0,1},{1,0},{2,3},{3,2},{4,5},{5,4},{6,7},{7,6},{8,9},{9,8},{10,11... | collective-permute-start | bytes 3686408 | tf_op jit(solution)/shard_map/ppermute | solution.py:589
  317.8 13.9 %collective-permute-start.11 = (bf16[3,64,3200]{2,1,0:T(8,128)(2,1)}, bf16[3,64,3200]{2,1,0:T(8,128)(2,1)}, u32[]{:S(2)}, u32[]{:S(2)}) collective-permute-start(bf16[3,64,3200]{2,1,0:T(8,128)(2,1)} %collective-permute-done.9.refs_2_), channel_id=1, source_target_pairs={{0,1},{1,0},{2,3},{3,2},{4,5},{5,4},{6,7},{7,6},{8,9},{9,8},{10,11... | collective-permute-start | bytes 3686408 | tf_op jit(solution)/shard_map/ppermute | solution.py:589
  318.3 29.3 %collective-permute-start.12 = (bf16[3,64,3200]{2,1,0:T(8,128)(2,1)}, bf16[3,64,3200]{2,1,0:T(8,128)(2,1)}, u32[]{:S(2)}, u32[]{:S(2)}) collective-permute-start(bf16[3,64,3200]{2,1,0:T(8,128)(2,1)} %get-tuple-element.148.refs_4_), channel_id=1, source_target_pairs={{0,2},{1,3},{2,0},{3,1},{4,6},{5,7},{6,4},{7,5},{8,10},{9,11},{10,... | collective-permute-start | bytes 3686408 | tf_op jit(solution)/shard_map/ppermute | solution.py:580
  318.9 30.3 %collective-permute-start.13 = (bf16[3,64,3200]{2,1,0:T(8,128)(2,1)}, bf16[3,64,3200]{2,1,0:T(8,128)(2,1)}, u32[]{:S(2)}, u32[]{:S(2)}) collective-permute-start(bf16[3,64,3200]{2,1,0:T(8,128)(2,1)} %get-tuple-element.148.refs_4_), channel_id=1, source_target_pairs={{0,6},{1,7},{2,4},{3,5},{4,2},{5,3},{6,0},{7,1},{8,14},{9,15},{10,... | collective-permute-start | bytes 3686408 | tf_op jit(solution)/shard_map/ppermute | solution.py:581
  349.2 13.3 %collective-permute-start.14 = (bf16[3,64,3200]{2,1,0:T(8,128)(2,1)}, bf16[3,64,3200]{2,1,0:T(8,128)(2,1)S(1)}, u32[]{:S(2)}, u32[]{:S(2)}) collective-permute-start(bf16[3,64,3200]{2,1,0:T(8,128)(2,1)} %collective-permute-done.12.refs_1_), channel_id=1, source_target_pairs={{0,1},{1,0},{2,3},{3,2},{4,5},{5,4},{6,7},{7,6},{8,9},{9,8},{10,11... | collective-permute-start | bytes 3686408 | tf_op jit(solution)/shard_map/ppermute | solution.py:589
  349.2 13.3 %collective-permute-start.15 = (bf16[3,64,3200]{2,1,0:T(8,128)(2,1)}, bf16[3,64,3200]{2,1,0:T(8,128)(2,1)}, u32[]{:S(2)}, u32[]{:S(2)}) collective-permute-start(bf16[3,64,3200]{2,1,0:T(8,128)(2,1)} %collective-permute-done.13.refs_2_), channel_id=1, source_target_pairs={{0,1},{1,0},{2,3},{3,2},{4,5},{5,4},{6,7},{7,6},{8,9},{9,8},{10,11... | collective-permute-start | bytes 3686408 | tf_op jit(solution)/shard_map/ppermute | solution.py:589
  349.7 30.5 %collective-permute-start.17 = (bf16[3,64,3200]{2,1,0:T(8,128)(2,1)}, bf16[3,64,3200]{2,1,0:T(8,128)(2,1)}, u32[]{:S(2)}, u32[]{:S(2)}) collective-permute-start(bf16[3,64,3200]{2,1,0:T(8,128)(2,1)} %collective-permute-done.2.refs_1_), channel_id=1, source_target_pairs={{0,6},{1,7},{2,4},{3,5},{4,2},{5,3},{6,0},{7,1},{8,14},{9,15},{10,... | collective-permute-start | bytes 3686408 | tf_op jit(solution)/shard_map/ppermute | solution.py:588
  351.7 29.0 %collective-permute-start.16 = (bf16[3,64,3200]{2,1,0:T(8,128)(2,1)}, bf16[3,64,3200]{2,1,0:T(8,128)(2,1)}, u32[]{:S(2)}, u32[]{:S(2)}) collective-permute-start(bf16[3,64,3200]{2,1,0:T(8,128)(2,1)} %collective-permute-done.1.refs_2_), channel_id=1, source_target_pairs={{0,2},{1,3},{2,0},{3,1},{4,6},{5,7},{6,4},{7,5},{8,10},{9,11},{10,... | collective-permute-start | bytes 3686408 | tf_op jit(solution)/shard_map/ppermute | solution.py:588
  380.6 12.8 %collective-permute-start.18 = (bf16[3,64,3200]{2,1,0:T(8,128)(2,1)}, bf16[3,64,3200]{2,1,0:T(8,128)(2,1)S(1)}, u32[]{:S(2)}, u32[]{:S(2)}) collective-permute-start(bf16[3,64,3200]{2,1,0:T(8,128)(2,1)} %collective-permute-done.16.refs_1_), channel_id=1, source_target_pairs={{0,1},{1,0},{2,3},{3,2},{4,5},{5,4},{6,7},{7,6},{8,9},{9,8},{10,11... | collective-permute-start | bytes 3686408 | tf_op jit(solution)/shard_map/ppermute | solution.py:596
  380.6 12.9 %collective-permute-start.19 = (bf16[3,64,3200]{2,1,0:T(8,128)(2,1)}, bf16[3,64,3200]{2,1,0:T(8,128)(2,1)}, u32[]{:S(2)}, u32[]{:S(2)}) collective-permute-start(bf16[3,64,3200]{2,1,0:T(8,128)(2,1)} %collective-permute-done.17.refs_2_), channel_id=1, source_target_pairs={{0,1},{1,0},{2,3},{3,2},{4,5},{5,4},{6,7},{7,6},{8,9},{9,8},{10,11... | collective-permute-start | bytes 3686408 | tf_op jit(solution)/shard_map/ppermute | solution.py:596
  381.1 29.2 %collective-permute-start.20 = (bf16[3,64,3200]{2,1,0:T(8,128)(2,1)}, bf16[3,64,3200]{2,1,0:T(8,128)(2,1)}, u32[]{:S(2)}, u32[]{:S(2)}) collective-permute-start(bf16[3,64,3200]{2,1,0:T(8,128)(2,1)} %collective-permute-done.9.refs_2_), channel_id=1, source_target_pairs={{0,2},{1,3},{2,0},{3,1},{4,6},{5,7},{6,4},{7,5},{8,10},{9,11},{10,... | collective-permute-start | bytes 3686408 | tf_op jit(solution)/shard_map/ppermute | solution.py:588
  381.4 30.2 %collective-permute-start.21 = (bf16[3,64,3200]{2,1,0:T(8,128)(2,1)}, bf16[3,64,3200]{2,1,0:T(8,128)(2,1)}, u32[]{:S(2)}, u32[]{:S(2)}) collective-permute-start(bf16[3,64,3200]{2,1,0:T(8,128)(2,1)} %collective-permute-done.12.refs_1_), channel_id=1, source_target_pairs={{0,6},{1,7},{2,4},{3,5},{4,2},{5,3},{6,0},{7,1},{8,14},{9,15},{10,... | collective-permute-start | bytes 3686408 | tf_op jit(solution)/shard_map/ppermute | solution.py:588
  411.6 11.3 %collective-permute-start.22 = (bf16[3,64,3200]{2,1,0:T(8,128)(2,1)}, bf16[3,64,3200]{2,1,0:T(8,128)(2,1)S(1)}, u32[]{:S(2)}, u32[]{:S(2)}) collective-permute-start(bf16[3,64,3200]{2,1,0:T(8,128)(2,1)} %collective-permute-done.20.refs_1_), channel_id=1, source_target_pairs={{0,1},{1,0},{2,3},{3,2},{4,5},{5,4},{6,7},{7,6},{8,9},{9,8},{10,11... | collective-permute-start | bytes 3686408 | tf_op jit(solution)/shard_map/ppermute | solution.py:596
  411.6 11.3 %collective-permute-start.23 = (bf16[3,64,3200]{2,1,0:T(8,128)(2,1)}, bf16[3,64,3200]{2,1,0:T(8,128)(2,1)}, u32[]{:S(2)}, u32[]{:S(2)}) collective-permute-start(bf16[3,64,3200]{2,1,0:T(8,128)(2,1)} %collective-permute-done.21.refs_2_), channel_id=1, source_target_pairs={{0,1},{1,0},{2,3},{3,2},{4,5},{5,4},{6,7},{7,6},{8,9},{9,8},{10,11... | collective-permute-start | bytes 3686408 | tf_op jit(solution)/shard_map/ppermute | solution.py:596
  (5 other events, 5.3 us)
